TPU v7x, 256 devices: a whole 4x4x8 slice. The times are simulated.
256 devices in a mesh: depth: 32 (over y, z_lo, core), chan: 8 (over x, z_hi).
Axes of the slice: x: 4, y: 4, z: 8 (z_hi: 2, z_lo: 4; z = z_hi * 4 + z_lo), core: 2. Of those that a mesh axis runs over, the one named last changes fastest.
Arguments:
- pre: float32 [1, 512, 64, 256], P(None, 'chan', 'depth'), may hold values from -6 to 6
- grad_out: float32 [1, 512, 64, 256], P(None, 'chan', 'depth'), may hold values from -6 to 6
- weight: float32 [27, 512, 512], P(None, 'chan'), may hold values from -0.0546875 to 0.0546875
Outputs:
- grad_pre: float32 [1, 512, 64, 256], P(None, 'chan', 'depth')
- grad_weight: float32 [27, 512, 512], P(None, 'chan', 'depth')
All inputs are finite; a program needn't handle non-finite values.
Results may differ from a plain program's by a relative error of at most 0.0001.
Values sent between devices are 32-bit elements; how exact they have to be, the bound alone decides.
No kernel may reach another device: no remote copies, remote signals or barrier semaphores. Data moves between devices by JAX's collectives and lax.ppermute only.
A program may use at most 192 MiB of HBM per device.

v0:
```python
import math

import jax
import jax.numpy as jnp
from jax import lax
from jax.sharding import PartitionSpec as P

W = 16


def with_halo(x, sides, width):
    for axis, dim in sides:
        size, length = (lax.axis_size(axis), x.shape[dim])
        up = [(i, (i + 1) % size) for i in range(size - 1)]
        down = [(j, i) for i, j in up]
        last = lax.slice_in_dim(x, length - width, length, axis=dim)
        first = lax.slice_in_dim(x, 0, width, axis=dim)
        before = lax.ppermute(last, axis, up)
        after = lax.ppermute(first, axis, down)
        x = jnp.concatenate([before, x, after], axis=dim)
    return x


def laid_out(tiles, dim):
    tiles = jnp.moveaxis(tiles, 0, dim)
    shape = tiles.shape
    return tiles.reshape(*shape[:dim], shape[dim] * shape[dim + 1], *shape[dim + 2 :])


def from_everyone(x, axis):
    length = lax.axis_size(axis)
    return lax.all_to_all(jnp.broadcast_to(x[None], (length, *x.shape)), axis, 0, 0, tiled=True)


def collect(x, axis, dim):
    return laid_out(from_everyone(x, axis), dim)


def shift_plane(block, drow, dcol):
    plane = block.shape[-1]
    step = drow * W + dcol
    lead = [(0, 0)] * (block.ndim - 1)
    if step > 0:
        moved = jnp.pad(block[..., step:], lead + [(0, step)])
    elif step < 0:
        moved = jnp.pad(block[..., : plane + step], lead + [(-step, 0)])
    else:
        moved = block
    column = jnp.arange(plane) % W
    valid = (column + dcol >= 0) & (column + dcol < W)
    return jnp.where(valid, moved, jnp.float32(0.0))


def normal_cdf(value):
    return 0.5 * (1.0 + jax.scipy.special.erf(value / math.sqrt(2.0)))


def transposed(weight, padded_piece, out_planes):
    total = jnp.zeros(
        (padded_piece.shape[0], weight.shape[1], out_planes, padded_piece.shape[3]), jnp.float32
    )
    for depth_off in range(3):
        layer = padded_piece[:, :, 2 - depth_off : 2 - depth_off + out_planes]
        for row_off in range(3):
            moved = jnp.stack(
                [shift_plane(layer, 1 - row_off, 1 - col_off) for col_off in range(3)]
            )
            first = 9 * depth_off + 3 * row_off
            total = total + jnp.einsum(
                "kco,kbodp->bcdp", weight[first : first + 3], moved, precision=lax.Precision.HIGHEST
            )
    return total


def shards(pre, grad_out, weight):
    batch, width_blk, planes, plane = pre.shape
    padded_pre = with_halo(pre, (("depth", 2),), 1)
    act = padded_pre * normal_cdf(padded_pre)
    sources = jnp.stack(
        [
            shift_plane(act[:, :, kd : kd + planes], kh - 1, kw - 1)
            for kd in range(3)
            for kh in range(3)
            for kw in range(3)
        ]
    )
    whole = collect(grad_out, "chan", 1)
    rimmed = with_halo(whole, (("depth", 2),), 1)
    grad_act = transposed(weight, rimmed, planes)
    filt = jnp.einsum("kbcdp,bodp->kco", sources, whole, precision=lax.Precision.HIGHEST)
    slope = normal_cdf(pre) + pre * jnp.exp(-0.5 * pre * pre) / math.sqrt(2.0 * math.pi)
    grad_pre = grad_act * slope
    summed = lax.psum_scatter(filt, "depth", scatter_dimension=2, tiled=True)
    voxel_count = batch * planes * lax.axis_size("depth") * plane
    grad_weight = summed * float(voxel_count) ** (-0.5)
    return (grad_pre, grad_weight)


def solution(mesh):
    placed = (P(None, "chan", "depth", None), P(None, "chan", "depth", None), P(None, "chan", None))
    return jax.shard_map(
        shards,
        mesh=mesh,
        in_specs=placed,
        out_specs=(P(None, "chan", "depth", None), P(None, "chan", "depth")),
        check_vma=False,
    )
```

profile of v0, /device:TPU:2, one launch (start us, length us, event | category | flops | bytes accessed | tf_op | source)
XLA Modules:
  0.0 238.3 jit_solution(15167546393344435964)
XLA Ops:
  7.2 1.2 fusion.135
  8.3 1.7 collective-permute-start.2
  10.1 1.3 collective-permute-start.3
  12.3 1.1 broadcast_in_dim.236
  13.4 11.5 %all-to-all-start = ((f32[8,1,64,2,256]{4,2,3,1,0:T(8,128)}), f32[8,1,64,2,256]{4,2,3,1,0:T(8,128)S(1)}, u32[]{:S(2)}, u32[]{:S(2)}) async-start(f32[8,1,64,2,256]{4,2,3,1,0:T(8,128)} %broadcast_in_dim.236), calls=%async_computation | async-start | bytes 2097152 | tf_op jit(solution)/shard_map/all_to_all | solution.py:32
  44.8 15.5 %fusion.47 = f32[27,64,512]{1,2,0:T(8,128)} fusion(f32[512,2,256,1]{2,0,1,3:T(8,128)S(1)} %bitcast.337, f32[27,1,64,2,256]{4,2,3,0,1:T(8,128)} %bitcast_dynamic-update-slice_fusion.23), kind=kOutput, calls=%fused_computation.72 | convolution fusion | flops 5435817984 | bytes 8126464 | tf_op jit(solution)/shard_map/kbcdp,bodp->kco/dot_general | solution.py:90
  60.5 1.3 collective-permute-start
  61.8 13.1 %collective-permute-start.1 = (f32[1,512,1,256]{3,1,2,0:T(8,128)S(1)}, f32[1,512,1,256]{3,1,2,0:T(8,128)S(1)}, u32[]{:S(2)}, u32[]{:S(2)}) collective-permute-start(f32[1,512,1,256]{3,1,2,0:T(8,128)S(1)} %get-tuple-element.41), channel_id=1, source_target_pairs={{0,8},{8,16},{16,24},{24,32},{32,40},{40,48},{48,56},{56,64},{64,7... | collective-permute-start | bytes 1572872 | tf_op jit(solution)/shard_map/ppermute | solution.py:18
  74.8 1.1 bitcast_select_fusion
  76.1 2.8 %fusion.80 = (f32[1,512,2,239]{3,1,2,0:T(8,128)}, f32[1,512,2,239]{3,1,2,0:T(8,128)}, f32[1,512,2,239]{3,1,2,0:T(8,128)}, f32[1,512,2,239]{3,1,2,0:T(8,128)}) fusion(f32[1,512,2,256]{3,1,2,0:T(8,128)S(1)} %bitcast.339, f32[1,512,1,256]{3,1,2,0:T(8,128)S(1)} %collective-permute-done, f32[1,512,1,256]{3,1,2,0:T(8,128)S(1)} %collective-permute-done.1), kind=kLoop, calls=%fused_computation.119 | loop fusion | flops 489472 | bytes 8110080 | tf_op jit(solution)/shard_map/concatenate | solution.py:20
  80.0 3.6 %select_bitcast_fusion.20 = (f32[1,1,512,2,256]{4,2,0,3,1:T(8,128)}, f32[1,1,512,2,256]{4,2,3,1,0:T(8,128)}, f32[1,1,512,2,256]{4,2,3,1,0:T(8,128)}, f32[1,1,512...) fusion(f32[1,512,2,240]{3,1,2,0:T(8,128)S(1)} %get-tuple-element.10, ...), kind=kLoop, calls=%fused_computation.156 | loop fusion | flops 1572864 | bytes 12189952 | tf_op jit(solution)/shard_map/stack | solution.py:65
  85.8 6.2 %select_bitcast_fusion.18 = (f32[1,1,512,2,256]{4,2,3,1,0:T(8,128)S(1)}, f32[1,1,512,2,256]{4,2,3,1,0:T(8,128)}, f32[1,1,512,2,256]{4,2,3,1,0:T(8,128)}, f32[1,1...) fusion(f32[1,512,2,255]{3,1,2,0:T(8,128)S(1)} %get-tuple-elemen, ...), kind=kLoop, calls=%fused_computation.154 | loop fusion | flops 2359296 | bytes 18469120 | tf_op jit(solution)/shard_map/stack | solution.py:65
  92.0 3.8 %fusion.76 = (f32[1,1,512,2,256]{4,2,3,1,0:T(8,128)S(1)}, f32[1,1,512,2,256]{4,2,3,1,0:T(8,128)S(1)}, f32[1,1,512,2,256]{4,2,3,1,0:T(8,128)S(1)}, f32[1,1,512,2,...) fusion(f32[1,512,2,256]{3,1,2,0:T(8,128)S(1)} %bitcast.343, ...), kind=kLoop, calls=%fused_computation.115 | loop fusion | flops 5242880 | bytes 20705792 | tf_op jit(solution)/shard_map/stack | solution.py:65
  95.8 2.1 fusion.58
  98.0 2.1 fusion.56
  100.2 2.1 fusion.55
  102.4 2.1 fusion.54
  104.5 2.1 fusion.53
  106.7 2.1 fusion.52
  108.9 2.4 %fusion.51 = f32[2,256,64]{1,2,0:T(8,128)S(1)} fusion(f32[1,1,512,2,256]{4,2,3,1,0:T(8,128)S(1)} %get-tuple-element.74, f32[1,1,512,2,256]{4,2,3,1,0:T(8,128)S(1)} %get-tuple-element.20, f32[1,1,512,2,256]{4,2,3,1,0:T(8,128)S(1)} %copy-done.9, f32[27,64,512]{2,1,0:T(8,128)S(1)} %copy-done.16), kind=kOutput, calls=%fused_computation.90 | convolution fusion | flops 605552640 | bytes 3670016 | tf_op jit(solution)/shard_map/kco,kbodp->bcdp/dot_general | solution.py:69
  111.3 2.1 fusion.50
  113.4 2.2 fusion.68
  116.4 113.5 %reduce-scatter.2.cloned.1.call-done = f32[27,64,16]{1,2,0:T(8,128)} async-done(((f32[27,64,512]{1,2,0:T(8,128)}), f32[27,64,16]{1,2,0:T(8,128)}) %reduce-scatter.2.cloned.1.call-update) | async-done | bytes 110608 | tf_op jit(solution)/shard_map/reduce_scatter | solution.py:93
  229.8 1.6 broadcast_multiply_fusion
  (87 shorter events, 25.1 us)
Async XLA Ops:
  7.2 17.8 %copy-start = (f32[1,64,2,256]{3,2,1,0:T(2,128)S(1)}, f32[1,64,2,256]{3,2,1,0:T(2,128)}, u32[]{:S(2)}) copy-start(f32[1,64,2,256]{3,2,1,0:T(2,128)} %param.3) | copy-start | bytes 393220
  8.3 16.5 %collective-permute-start.2 = (f32[1,64,1,256]{3,1,2,0:T(8,128)S(1)}, f32[1,64,1,256]{3,1,2,0:T(8,128)S(1)}, u32[]{:S(2)}, u32[]{:S(2)}) collective-permute-start(f32[1,64,1,256]{3,1,2,0:T(8,128)S(1)} %copy.118), channel_id=1, source_target_pairs={{0,8},{8,16},{16,24},{24,32},{32,40},{40,48},{48,56},{56,64},{64,7... | collective-permute-start | bytes 196616 | tf_op jit(solution)/shard_map/ppermute | solution.py:18
  10.1 14.8 %collective-permute-start.3 = (f32[1,64,1,256]{3,1,2,0:T(8,128)S(1)}, f32[1,64,1,256]{3,1,2,0:T(8,128)S(1)}, u32[]{:S(2)}, u32[]{:S(2)}) collective-permute-start(f32[1,64,1,256]{3,1,2,0:T(8,128)S(1)} %copy.119), channel_id=1, source_target_pairs={{8,0},{16,8},{24,16},{32,24},{40,32},{48,40},{56,48},{64,56},{72,6... | collective-permute-start | bytes 196616 | tf_op jit(solution)/shard_map/ppermute | solution.py:19
  13.4 31.3 %all-to-all-start = ((f32[8,1,64,2,256]{4,2,3,1,0:T(8,128)}), f32[8,1,64,2,256]{4,2,3,1,0:T(8,128)S(1)}, u32[]{:S(2)}, u32[]{:S(2)}) async-start(f32[8,1,64,2,256]{4,2,3,1,0:T(8,128)} %broadcast_in_dim.236), calls=%async_computation | async-start | bytes 2097152 | tf_op jit(solution)/shard_map/all_to_all | solution.py:32
  24.9 205.0 %reduce-scatter.2.cloned.1.call-start = ((), (), s32[]{:S(2)}) async-start(), calls=%async_computation.2 | async-start | bytes 7299072 | tf_op jit(solution)/shard_map/reduce_scatter | solution.py:93
  60.5 15.5 %collective-permute-start = (f32[1,512,1,256]{3,1,2,0:T(8,128)S(1)}, f32[1,512,1,256]{3,1,2,0:T(8,128)S(1)}, u32[]{:S(2)}, u32[]{:S(2)}) collective-permute-start(f32[1,512,1,256]{3,1,2,0:T(8,128)S(1)} %get-tuple-element.40), channel_id=1, source_target_pairs={{8,0},{16,8},{24,16},{32,24},{40,32},{48,40},{56,48},{64,56},{72,6... | collective-permute-start | bytes 1572872 | tf_op jit(solution)/shard_map/ppermute | solution.py:19
  61.8 14.4 %collective-permute-start.1 = (f32[1,512,1,256]{3,1,2,0:T(8,128)S(1)}, f32[1,512,1,256]{3,1,2,0:T(8,128)S(1)}, u32[]{:S(2)}, u32[]{:S(2)}) collective-permute-start(f32[1,512,1,256]{3,1,2,0:T(8,128)S(1)} %get-tuple-element.41), channel_id=1, source_target_pairs={{0,8},{8,16},{16,24},{24,32},{32,40},{40,48},{48,56},{56,64},{64,7... | collective-permute-start | bytes 1572872 | tf_op jit(solution)/shard_map/ppermute | solution.py:18
  92.0 3.8 %copy-start.6 = (f32[1,1,512,2,256]{4,2,0,3,1:T(8,128)S(1)}, f32[1,1,512,2,256]{4,2,0,3,1:T(8,128)}, u32[]{:S(2)}) copy-start(f32[1,1,512,2,256]{4,2,0,3,1:T(8,128)} %get-tuple-element.84) | copy-start | bytes 3145732
  92.0 3.8 %copy-start.15 = (f32[1,1,512,2,256]{4,2,0,3,1:T(8,128)S(1)}, f32[1,1,512,2,256]{4,2,0,3,1:T(8,128)}, u32[]{:S(2)}) copy-start(f32[1,1,512,2,256]{4,2,0,3,1:T(8,128)} %get-tuple-element.83) | copy-start | bytes 3145732
  92.0 3.8 %copy-start.16 = (f32[27,64,512]{2,1,0:T(8,128)S(1)}, f32[27,64,512]{2,1,0:T(8,128)}, u32[]{:S(2)}) copy-start(f32[27,64,512]{2,1,0:T(8,128)} %param.5) | copy-start | bytes 10616836
  95.8 2.2 copy-start.5
  95.8 2.2 copy-start.14
  95.8 4.3 %copy-start.4 = (f32[1,1,512,2,256]{4,2,3,1,0:T(8,128)S(1)}, f32[1,1,512,2,256]{4,2,3,1,0:T(8,128)}, u32[]{:S(2)}) copy-start(f32[1,1,512,2,256]{4,2,3,1,0:T(8,128)} %get-tuple-element.86) | copy-start | bytes 3145732
  95.8 4.3 %copy-start.13 = (f32[1,1,512,2,256]{4,2,3,1,0:T(8,128)S(1)}, f32[1,1,512,2,256]{4,2,3,1,0:T(8,128)}, u32[]{:S(2)}) copy-start(f32[1,1,512,2,256]{4,2,3,1,0:T(8,128)} %get-tuple-element.77) | copy-start | bytes 3145732
  98.0 4.3 %copy-start.7 = (f32[1,1,512,2,256]{4,2,3,1,0:T(8,128)S(1)}, f32[1,1,512,2,256]{4,2,3,1,0:T(8,128)}, u32[]{:S(2)}) copy-start(f32[1,1,512,2,256]{4,2,3,1,0:T(8,128)} %bitcast_select_fusion) | copy-start | bytes 3145732
  98.0 4.3 %copy-start.12 = (f32[1,1,512,2,256]{4,2,3,1,0:T(8,128)S(1)}, f32[1,1,512,2,256]{4,2,3,1,0:T(8,128)}, u32[]{:S(2)}) copy-start(f32[1,1,512,2,256]{4,2,3,1,0:T(8,128)} %get-tuple-element.78) | copy-start | bytes 3145732
  100.2 4.3 %copy-start.3 = (f32[1,1,512,2,256]{4,2,3,1,0:T(8,128)S(1)}, f32[1,1,512,2,256]{4,2,3,1,0:T(8,128)}, u32[]{:S(2)}) copy-start(f32[1,1,512,2,256]{4,2,3,1,0:T(8,128)} %get-tuple-element.87) | copy-start | bytes 3145732
  100.2 4.3 %copy-start.11 = (f32[1,1,512,2,256]{4,2,3,1,0:T(8,128)S(1)}, f32[1,1,512,2,256]{4,2,3,1,0:T(8,128)}, u32[]{:S(2)}) copy-start(f32[1,1,512,2,256]{4,2,3,1,0:T(8,128)} %get-tuple-element.79) | copy-start | bytes 3145732
  102.3 4.3 %copy-start.2 = (f32[1,1,512,2,256]{4,2,3,1,0:T(8,128)S(1)}, f32[1,1,512,2,256]{4,2,3,1,0:T(8,128)}, u32[]{:S(2)}) copy-start(f32[1,1,512,2,256]{4,2,3,1,0:T(8,128)} %get-tuple-element.88) | copy-start | bytes 3145732
  102.4 4.3 %copy-start.10 = (f32[1,1,512,2,256]{4,2,3,1,0:T(8,128)S(1)}, f32[1,1,512,2,256]{4,2,3,1,0:T(8,128)}, u32[]{:S(2)}) copy-start(f32[1,1,512,2,256]{4,2,3,1,0:T(8,128)} %get-tuple-element.80) | copy-start | bytes 3145732
  104.5 4.3 %copy-start.9 = (f32[1,1,512,2,256]{4,2,3,1,0:T(8,128)S(1)}, f32[1,1,512,2,256]{4,2,3,1,0:T(8,128)}, u32[]{:S(2)}) copy-start(f32[1,1,512,2,256]{4,2,3,1,0:T(8,128)} %get-tuple-element.81) | copy-start | bytes 3145732
  106.7 4.6 %copy-start.1 = (f32[1,1,512,2,256]{4,2,3,1,0:T(8,128)S(1)}, f32[1,1,512,2,256]{4,2,3,1,0:T(8,128)}, u32[]{:S(2)}) copy-start(f32[1,1,512,2,256]{4,2,3,1,0:T(8,128)} %get-tuple-element.89) | copy-start | bytes 3145732
  106.7 4.6 %copy-start.8 = (f32[1,1,512,2,256]{4,2,3,1,0:T(8,128)S(1)}, f32[1,1,512,2,256]{4,2,3,1,0:T(8,128)}, u32[]{:S(2)}) copy-start(f32[1,1,512,2,256]{4,2,3,1,0:T(8,128)} %get-tuple-element.82) | copy-start | bytes 3145732
Sparse Core Ops, SparseCore 0:
  60.5 169.2 reduce-scatter.1
where the time goes:
time: 239 us; the launch traced here: 238 us
  waiting for transfers between devices  114 us (48%)
  other arithmetic  41.4 us (17%)
  matrix products  35.1 us (15%)
  starting transfers between devices  28.8 us (12%)
  between operations  14.4 us (6%)
  local copies, waits for them, and re-layouts  4.87 us (2%)
    reduce_scatter x1, waiting for transfers between devices, shards(): summed = lax.psum_scatter(filt, 'depth', scatter_dimension=2, tiled=True)  113 us
    dot_general x9, matrix products, transposed(): jnp.einsum('kco,kbodp->bcdp', weight[first:first + 3], moved, precision=l...  19.6 us
    unnamed x26, other arithmetic  18.3 us
    dot_general x1, matrix products, shards(): jnp.einsum('kbcdp,bodp->kco', sources, whole, precision=lax.Precision.HIG...  15.5 us
    ppermute x2, starting transfers between devices, with_halo(): before = lax.ppermute(last, axis, up)  14.8 us
    another operation x3, other arithmetic, transposed(): jnp.stack([shift_plane(layer, 1 - row_off, 1 - col_off) for col_off in ra...  13.6 us
    all_to_all x1, starting transfers between devices, from_everyone(): lax.all_to_all(jnp.broadcast_to(x[None], (length, *x.shape)), axis, 0, 0,...  11.5 us
    concatenate x4, other arithmetic, with_halo(): x = jnp.concatenate([before, x, after], axis=dim)  6.02 us
  transfers between devices with their start and end apart: 6, of which 2 were waited for; matrix products, arithmetic and copies ran while one was open for 26% of the time, Pallas kernels for 0%

commit v1 on v0

v1 whole, which is shorter than its diff:
```python
import math

import jax
import jax.numpy as jnp
from jax import lax
from jax.experimental import pallas as pl
from jax.experimental.pallas import tpu as pltpu
from jax.sharding import Mesh, PartitionSpec as P


W = 16
CELLS = 256
TAPS = 576
LANES = 1792
GRANT = 24 * 1024 * 1024
DEPTH_AXES = ("y", "zl", "core")
NT = (((1,), (1,)), ((), ()))
NN = (((1,), (0,)), ((), ()))


def normal_cdf(value):
    return 0.5 * (1.0 + jax.scipy.special.erf(value / math.sqrt(2.0)))


def split(value):
    hi = value.astype(jnp.bfloat16)
    lo = (value - hi.astype(jnp.float32)).astype(jnp.bfloat16)
    return hi, lo


def mul(a, b, dims):
    return lax.dot_general(a, b, dims, preferred_element_type=jnp.float32)


def moved(block, step):
    return block if step == 0 else pltpu.roll(block, (-step) % CELLS, 1)


def col_ok(shape, dcol):
    column = lax.broadcasted_iota(jnp.int32, shape, 1) % W
    return (column + dcol >= 0) & (column + dcol < W)


def row_ok(shape, drow):
    row = lax.broadcasted_iota(jnp.int32, shape, 1) // W
    return (row + drow >= 0) & (row + drow < CELLS // W)


def shift_cols(block, dcol):
    if dcol == 0:
        return block
    return jnp.where(col_ok(block.shape, dcol), moved(block, dcol), 0.0)


def shift_rows(block, drow):
    if drow == 0:
        return block
    return jnp.where(row_ok(block.shape, drow), moved(block, drow * W), 0.0)


def call(kernel, out_shapes, n_in, scratch=(), flops=0, moved_bytes=0):
    vmem = pl.BlockSpec(memory_space=pltpu.VMEM)
    return pl.pallas_call(
        kernel,
        out_shape=out_shapes,
        in_specs=[pl.BlockSpec(memory_space=pltpu.SMEM)] + [vmem] * n_in,
        out_specs=jax.tree.map(lambda _: vmem, out_shapes),
        scratch_shapes=scratch,
        cost_estimate=pl.CostEstimate(flops=flops, bytes_accessed=moved_bytes, transcendentals=0),
        compiler_params=pltpu.CompilerParams(vmem_limit_bytes=GRANT),
    )


def weight_kernel(ids, w_ref, hi_ref, lo_ref):
    core = ids[2]
    even = (lax.broadcasted_iota(jnp.int32, (64, 128), 1) // 16) % 2 == 0

    def tap_body(tap, carry):
        rows = pl.ds(pl.multiple_of(64 * tap, 64), 64)
        for kd in range(3):
            for pair in range(2):
                first = w_ref[9 * kd + tap, :, 256 * pair : 256 * pair + 128]
                second = w_ref[9 * kd + tap, :, 256 * pair + 128 : 256 * pair + 256]
                low = jnp.where(even, first, pltpu.roll(second, 16, 1))
                high = jnp.where(even, pltpu.roll(first, 112, 1), second)
                hi, lo = split(jnp.where(core == 0, low, high))
                lanes = slice(256 * kd + 128 * pair, 256 * kd + 128 * pair + 128)
                hi_ref[rows, lanes] = hi
                lo_ref[rows, lanes] = lo
        return carry

    lax.fori_loop(0, 9, tap_body, 0)


def pick_weights(ids, weight):
    shape = jax.ShapeDtypeStruct((TAPS, 3 * CELLS), jnp.bfloat16)
    return call(weight_kernel, (shape, shape), 1, flops=200000000, moved_bytes=5000000)(ids, weight)


def act_kernel(ids, own, sib, edge, far_edge, hi_ref, lo_ref):
    core = ids[2]
    planes = [
        (own[0], 1 + 2 * core),
        (own[1], 2 + 2 * core),
        (sib[0], 3 - 2 * core),
        (sib[1], 4 - 2 * core),
        (edge[...], 5 * core),
        (far_edge[...], 5 - 5 * core),
    ]
    for block, place in planes:
        for dcol in (-1, 0, 1):
            cols = shift_cols(block, dcol)
            for drow in (-1, 0, 1):
                hi, lo = split(shift_rows(cols, drow))
                tap = 3 * (drow + 1) + dcol + 1
                rows = pl.ds(pl.multiple_of(TAPS * place + 64 * tap, 64), 64)
                hi_ref[rows, :] = hi
                lo_ref[rows, :] = lo
    hi_ref[6 * TAPS :, :] = jnp.zeros((64, CELLS), jnp.bfloat16)
    lo_ref[6 * TAPS :, :] = jnp.zeros((64, CELLS), jnp.bfloat16)


def expand_act(ids, own, sib, edge, far_edge):
    shape = jax.ShapeDtypeStruct((6 * TAPS + 64, CELLS), jnp.bfloat16)
    return call(act_kernel, (shape, shape), 4, flops=50000000, moved_bytes=4000000)(
        ids, own, sib, edge, far_edge
    )


def filter_kernel(ids, b0, b1, b2, b3, ahi, alo, o0, o1, o2, o3, both):
    y, core, x = ids[0], ids[2], ids[3]
    for s, block in enumerate((b0, b1, b2, b3)):
        u = (x - s - y + 8) % 4
        rows = pl.ds(pl.multiple_of(32 * u, 32), 32)
        rows_lo = pl.ds(pl.multiple_of(128 + 32 * u, 32), 32)
        for j in range(4):
            q = (j + 2 * core) % 4
            hi, lo = split(block[j])
            both[q, rows, :] = hi
            both[q, rows_lo, :] = lo
    outs = (o0, o1, o2, o3)
    for n in range(LANES // 256):
        wide = jnp.zeros((256, 256), jnp.float32)
        narrow = jnp.zeros((128, 256), jnp.float32)
        for q in range(4):
            taps = slice(TAPS * q + 256 * n, TAPS * q + 256 * n + 256)
            wide += mul(both[q], ahi[taps, :], NT)
            narrow += mul(both[q, :128], alo[taps, :], NT)
        total = wide[:128] + wide[128:] + narrow
        for u in range(4):
            outs[u][:, 256 * n : 256 * n + 256] = total[32 * u : 32 * u + 32]


def filter_terms(ids, blocks, ahi, alo):
    shape = jax.ShapeDtypeStruct((32, LANES), jnp.float32)
    scratch = [pltpu.VMEM((4, 256, CELLS), jnp.bfloat16)]
    return call(
        filter_kernel, (shape,) * 4, 6, scratch, flops=1400000000, moved_bytes=5000000
    )(ids, *blocks, ahi, alo)


def grad_kernel(ids, *refs):
    blocks, (whi, wlo, keep, send, ghi, glo) = refs[:8], refs[8:]
    core, x, zh = ids[2], ids[3], ids[4]
    for n, block in enumerate(blocks):
        src_x = (x - n % 4 + 4) % 4
        src_zh = zh if n < 4 else 1 - zh
        base = 128 * (src_x // 2) + 64 * src_zh + 16 * (src_x % 2)
        for j in range(4):
            q = (j + 2 * core) % 4
            hi, lo = split(block[j])
            for b in range(2):
                rows = pl.ds(pl.multiple_of((3 - q) * 256 + base + 32 * b, 16), 16)
                ghi[rows, :] = hi[16 * b : 16 * b + 16]
                glo[rows, :] = lo[16 * b : 16 * b + 16]
    for p in range(6):
        first, last = max(0, p - 3), min(2, p)
        lanes = slice(256 * first, 256 * (last + 1))
        top = 256 * (3 - p + first)
        depth = slice(top, top + 256 * (last + 1 - first))
        total = None
        for kh in range(3):
            taps = slice(192 * kh, 192 * kh + 192)
            z = (
                mul(whi[taps, lanes], ghi[depth, :], NN)
                + mul(wlo[taps, lanes], ghi[depth, :], NN)
                + mul(whi[taps, lanes], glo[depth, :], NN)
            )
            part = (
                shift_cols(z[:64], 1) + z[64:128] + shift_cols(z[128:], -1)
            )
            part = shift_rows(part, 1 - kh)
            total = part if total is None else total + part
        m = min(p, 5 - p)
        mine = core == (1 if p >= 3 else 0)

        @pl.when(mine)
        def _():
            keep[m] = total

        @pl.when(jnp.logical_not(mine))
        def _():
            send[m] = total


def grad_terms(ids, blocks, whi, wlo):
    shape = jax.ShapeDtypeStruct((3, 64, CELLS), jnp.float32)
    scratch = [pltpu.VMEM((4 * 256, CELLS), jnp.bfloat16)] * 2
    return call(
        grad_kernel, (shape, shape), 10, scratch, flops=2800000000, moved_bytes=4000000
    )(ids, *blocks, whi, wlo)


def ring(n, step):
    return [(i, (i + step) % n) for i in range(n)]


def work(pre, grad_out, weight):
    y, zl, core, x, zh = [lax.axis_index(a) for a in ("y", "zl", "core", "x", "zh")]
    ids = jnp.stack([y, zl, core, x, zh]).astype(jnp.int32)
    swap = [(0, 1), (1, 0)]

    cot = jnp.moveaxis(grad_out[0], 1, 0).reshape(2, 2, 2, 16, CELLS)
    mine = lax.dynamic_index_in_dim(cot, core, 2, keepdims=False).reshape(2, 32, CELLS)
    theirs = lax.dynamic_index_in_dim(cot, 1 - core, 2, keepdims=False).reshape(2, 32, CELLS)
    cot4 = jnp.concatenate([mine, lax.ppermute(theirs, "core", swap)], axis=0)
    across = lax.ppermute(cot4, "zh", swap)
    near = [cot4] + [lax.ppermute(cot4, "x", ring(4, s)) for s in (1, 2, 3)]
    far = [across] + [lax.ppermute(across, "x", ring(4, s)) for s in (1, 2, 3)]

    source = jnp.moveaxis(pre[0], 1, 0)
    cdf = normal_cdf(source)
    slope = cdf + source * jnp.exp(-0.5 * source * source) / math.sqrt(2.0 * math.pi)
    act, slope = lax.optimization_barrier((source * cdf, slope))
    edge = lax.dynamic_index_in_dim(act, core, 0, keepdims=False)
    outward = []
    for chip in range(16):
        if chip < 15:
            outward.append((2 * chip + 1, 2 * chip + 2))
        if chip > 0:
            outward.append((2 * chip, 2 * chip - 1))
    sib = lax.ppermute(act, "core", swap)
    edge = lax.ppermute(edge, DEPTH_AXES, outward)
    far_edge = lax.ppermute(edge, "core", swap)

    whi, wlo = pick_weights(ids, weight)
    ahi, alo = expand_act(ids, act, sib, edge, far_edge)

    def over_y(parts):
        total = parts[0]
        for t in (1, 2, 3):
            total = total + lax.ppermute(parts[t], "y", ring(4, t))
        return total

    sum_near = over_y(filter_terms(ids, near, ahi, alo))
    sum_far = over_y(filter_terms(ids, far, ahi, alo))
    keep, send = grad_terms(ids, near + far, whi, wlo)

    both = jnp.stack([sum_near, sum_far]).reshape(4, 16, LANES)

    def part_for(t):
        z = (zl + t) % 4
        return lax.dynamic_index_in_dim(both, 2 * ((z // 2 + zh) % 2) + z % 2, 0, keepdims=False)

    total = part_for(0)
    for t in (1, 2, 3):
        total = total + lax.ppermute(part_for(t), "zl", ring(4, t))
    total = total * float(16384) ** (-0.5)
    grad_weight = total.reshape(16, 28, 64)[:, :27].transpose(1, 2, 0)

    got = keep + lax.ppermute(send, "core", swap)
    close = got[1] + lax.ppermute(got[0], DEPTH_AXES, outward)
    grad_act = jnp.where(core == 0, jnp.stack([close, got[2]]), jnp.stack([got[2], close]))
    grad_pre = jnp.moveaxis(grad_act * slope, 0, 1)[None]
    return (grad_pre, grad_weight)


def solution(mesh):
    fine = Mesh(mesh.devices.reshape(4, 4, 2, 4, 2), ("y", "zl", "core", "x", "zh"))
    chan, depth = ("x", "zh"), DEPTH_AXES
    return jax.shard_map(
        work,
        mesh=fine,
        in_specs=(P(None, chan, depth, None), P(None, chan, depth, None), P(None, chan, None)),
        out_specs=(P(None, chan, depth, None), P(None, chan, depth)),
        check_vma=False,
    )
```

time: 239 us -> 77.7 us (0.33)
  the two profiles are of different devices: /device:TPU:2 before, /device:TPU:1 now
where the time goes in v1:
time: 77.7 us; the launch traced here: 77.4 us
  starting transfers between devices  35.3 us (45%)
  waiting for transfers between devices  19.3 us (25%)
  Pallas kernels  16.1 us (21%)
  local copies, waits for them, and re-layouts  4.74 us (6%)
  other arithmetic  1.21 us (2%)
  between operations  0.84 us (1%)
    ppermute x6, starting transfers between devices, over_y(): total = total + lax.ppermute(parts[t], 'y', ring(4, t))  10.5 us
    ppermute x6, waiting for transfers between devices, over_y(): total = total + lax.ppermute(parts[t], 'y', ring(4, t))  9.82 us
    ppermute x3, waiting for transfers between devices, work(): total = total + lax.ppermute(part_for(t), 'zl', ring(4, t))  9.4 us
    pallas_call x1, Pallas kernels, grad_terms(): call(grad_kernel, (shape, shape), 10, scratch, flops=2800000000, moved_by...  6.24 us
    ppermute x1, starting transfers between devices, work(): across = lax.ppermute(cot4, 'zh', swap)  6.1 us
    pallas_call x2, Pallas kernels, filter_terms(): call(filter_kernel, (shape,) * 4, 6, scratch, flops=1400000000, moved_byt...  5.62 us
    ppermute x3, starting transfers between devices, work(): near = [cot4] + [lax.ppermute(cot4, 'x', ring(4, s)) for s in (1, 2, 3)]  4.82 us
    unnamed x6, local copies, waits for them, and re-layouts  3.59 us
  transfers between devices with their start and end apart: 22, of which 5 were waited for; matrix products, arithmetic and copies ran while one was open for 3% of the time, Pallas kernels for 21%

profile of v1, /device:TPU:1, one launch (start us, length us, event | category | flops | bytes accessed | tf_op | source)
XLA Modules:
  0.0 77.4 jit_solution(5902114090890102699)
XLA Ops:
  1.5 3.3 %collective-permute-start = (f32[2,32,256]{2,1,0:T(8,128)S(1)}, f32[2,32,256]{2,1,0:T(8,128)S(1)}, u32[]{:S(2)}, u32[]{:S(2)}) collective-permute-start(f32[2,32,256]{2,1,0:T(8,128)S(1)} %bitcast.69), channel_id=1, source_target_pairs={{0,8},{8,0},{1,9},{9,1},{2,10},{10,2},{3,11},{11,3},{4,12},{12,4},... | collective-permute-start | bytes 196616 | tf_op jit(solution)/shard_map/ppermute | solution.py:226
  5.9 2.2 %collective-permute-start.11 = (f32[64,256]{1,0:T(8,128)S(1)}, f32[64,256]{1,0:T(8,128)S(1)}, u32[]{:S(2)}, u32[]{:S(2)}) collective-permute-start(f32[64,256]{1,0:T(8,128)S(1)} %dynamic-slice_bitcast_fusion.3), channel_id=1, source_target_pairs={{8,16},{24,32},{16,8},{40,48},{32,24},{56,64},{48,40},{72,80},{64,... | collective-permute-start | bytes 196616 | tf_op jit(solution)/shard_map/ppermute | solution.py:243
  8.2 6.1 %collective-permute-start.4 = (f32[4,32,256]{2,1,0:T(8,128)S(1)}, f32[4,32,256]{2,1,0:T(8,128)S(1)}, u32[]{:S(2)}, u32[]{:S(2)}) collective-permute-start(f32[4,32,256]{2,1,0:T(8,128)S(1)} %pad_maximum_fusion.1.refs_0_.b0), channel_id=1, source_target_pairs={{0,1},{1,0},{2,3},{3,2},{4,5},{5,4},{6,7},{7,6},{8,9},{9,8},{10,11... | collective-permute-start | bytes 393224 | tf_op jit(solution)/shard_map/ppermute | solution.py:227
  14.3 1.2 %collective-permute-start.1 = (f32[4,32,256]{2,1,0:T(8,128)S(1)}, f32[4,32,256]{2,1,0:T(8,128)S(1)}, u32[]{:S(2)}, u32[]{:S(2)}) collective-permute-start(f32[4,32,256]{2,1,0:T(8,128)S(1)} %pad_maximum_fusion.1.refs_0_.b0), channel_id=1, source_target_pairs={{0,2},{2,4},{4,6},{6,0},{1,3},{3,5},{5,7},{7,1},{8,10},{10,12},{12... | collective-permute-start | bytes 393224 | tf_op jit(solution)/shard_map/ppermute | solution.py:228
  15.5 2.5 %collective-permute-start.2 = (f32[4,32,256]{2,1,0:T(8,128)S(1)}, f32[4,32,256]{2,1,0:T(8,128)S(1)}, u32[]{:S(2)}, u32[]{:S(2)}) collective-permute-start(f32[4,32,256]{2,1,0:T(8,128)S(1)} %pad_maximum_fusion.1.refs_0_.b0), channel_id=1, source_target_pairs={{0,4},{2,6},{4,0},{6,2},{1,5},{3,7},{5,1},{7,3},{8,12},{10,14},{12... | collective-permute-start | bytes 393224 | tf_op jit(solution)/shard_map/ppermute | solution.py:228
  17.9 1.2 %collective-permute-start.3 = (f32[4,32,256]{2,1,0:T(8,128)S(1)}, f32[4,32,256]{2,1,0:T(8,128)S(1)}, u32[]{:S(2)}, u32[]{:S(2)}) collective-permute-start(f32[4,32,256]{2,1,0:T(8,128)S(1)} %pad_maximum_fusion.1.refs_0_.b0), channel_id=1, source_target_pairs={{0,6},{2,0},{4,2},{6,4},{1,7},{3,1},{5,3},{7,5},{8,14},{10,8},{12,... | collective-permute-start | bytes 393224 | tf_op jit(solution)/shard_map/ppermute | solution.py:228
  19.2 2.0 %copy-done = f32[27,64,512]{2,1,0:T(8,128)S(1)} copy-done((f32[27,64,512]{2,1,0:T(8,128)S(1)}, f32[27,64,512]{2,1,0:T(8,128)}, u32[]{:S(2)}) %copy-start) | copy-done | bytes 3538968
  21.2 2.1 %shard_map.50 = (bf16[576,768]{1,0:T(8,128)(2,1)S(1)}, bf16[576,768]{1,0:T(8,128)(2,1)S(1)}) custom-call(s32[5]{0:T(128)S(1)} %stack.42.ids, f32[27,64,512]{2,1,0:T(8,128)S(1)} %copy-done), custom_call_target="tpu_custom_call" | custom-call | flops 200000000 | bytes 5000000 | tf_op jit(solution)/shard_map/pallas_call | solution.py:97
  23.3 2.1 %shard_map.52 = (bf16[3520,256]{1,0:T(8,128)(2,1)S(1)}, bf16[3520,256]{1,0:T(8,128)(2,1)S(1)}) custom-call(s32[5]{0:T(128)S(1)} %stack.42.ids, f32[2,64,256]{2,1,0:T(8,128)S(1)} %get-tuple-element.23.own, f32[2,64,256]{2,1,0:T(8,128)S(1)} %collective-permute-done.10.sib, f32[64,256]{1,0:T(8,128)S(1)} %collective-permute-done.11.edge, ...), custom_call_target="tpu_custom_call" | custom-call | flops 50000000 | bytes 4000000 | tf_op jit(solution)/shard_map/pallas_call | solution.py:125
  25.8 1.2 %collective-permute-start.6 = (f32[4,32,256]{2,1,0:T(8,128)S(1)}, f32[4,32,256]{2,1,0:T(8,128)S(1)}, u32[]{:S(2)}, u32[]{:S(2)}) collective-permute-start(f32[4,32,256]{2,1,0:T(8,128)S(1)} %collective-permute-done.4.refs_4_.b0), channel_id=1, source_target_pairs={{0,4},{2,6},{4,0},{6,2},{1,5},{3,7},{5,1},{7,3},{8,12},{10,14},{12... | collective-permute-start | bytes 393224 | tf_op jit(solution)/shard_map/ppermute | solution.py:229
  27.0 1.3 %collective-permute-start.7 = (f32[4,32,256]{2,1,0:T(8,128)S(1)}, f32[4,32,256]{2,1,0:T(8,128)S(1)}, u32[]{:S(2)}, u32[]{:S(2)}) collective-permute-start(f32[4,32,256]{2,1,0:T(8,128)S(1)} %collective-permute-done.4.refs_4_.b0), channel_id=1, source_target_pairs={{0,6},{2,0},{4,2},{6,4},{1,7},{3,1},{5,3},{7,5},{8,14},{10,8},{12,... | collective-permute-start | bytes 393224 | tf_op jit(solution)/shard_map/ppermute | solution.py:229
  28.3 2.8 %shard_map.53 = (f32[32,1792]{1,0:T(8,128)S(1)}, f32[32,1792]{1,0:T(8,128)S(1)}, f32[32,1792]{1,0:T(8,128)S(1)}, f32[32,1792]{1,0:T(8,128)S(1)}) custom-call(s32[5]{0:T(128)S(1)} %stack.42.ids, f32[4,32,256]{2,1,0:T(8,128)S(1)} %pad_maximum_fusion.1.refs_0_.b0, f32[4,32,256]{2,1,0:T(8,128)S(1)} %collective-permute-done.1.refs_1_.b1, ...), custom_call_target="tpu_custom_call" | custom-call | flops 1400000000 | bytes 5000000 | tf_op jit(solution)/shard_map/pallas_call | solution.py:157
  31.2 5.1 %collective-permute-start.15 = (f32[32,1792]{1,0:T(8,128)S(1)}, f32[32,1792]{1,0:T(8,128)S(1)}, u32[]{:S(2)}, u32[]{:S(2)}) collective-permute-start(f32[32,1792]{1,0:T(8,128)S(1)} %get-tuple-element.29), channel_id=1, source_target_pairs={{0,192},{64,0},{128,64},{192,128},{1,193},{65,1},{129,65},{193,129... | collective-permute-start | bytes 688136 | tf_op jit(solution)/shard_map/ppermute | solution.py:252
  36.3 1.6 %collective-permute-start.13 = (f32[32,1792]{1,0:T(8,128)S(1)}, f32[32,1792]{1,0:T(8,128)S(1)}, u32[]{:S(2)}, u32[]{:S(2)}) collective-permute-start(f32[32,1792]{1,0:T(8,128)S(1)} %get-tuple-element.27), channel_id=1, source_target_pairs={{0,64},{64,128},{128,192},{192,0},{1,65},{65,129},{129,193},{193,1... | collective-permute-start | bytes 688136 | tf_op jit(solution)/shard_map/ppermute | solution.py:252
  37.9 6.2 %shard_map.51 = (f32[3,64,256]{2,1,0:T(8,128)S(1)}, f32[3,64,256]{2,1,0:T(8,128)S(1)}) custom-call(s32[5]{0:T(128)S(1)} %stack.42.ids, f32[4,32,256]{2,1,0:T(8,128)S(1)} %pad_maximum_fusion.1.refs_0_.b0, f32[4,32,256]{2,1,0:T(8,128)S(1)} %collective-permute-done.1.refs_1_.b1, f32[4,32,256]{2,1,0:T(8,128)S(1)} %collective-permute-done.2.refs_2_.b2, ...), custom_call_target="tpu_custom_call" | custom-call | flops 2800000000 | bytes 4000000 | tf_op jit(solution)/shard_map/pallas_call | solution.py:209
  44.1 1.2 %collective-permute-start.8 = (f32[3,64,256]{2,1,0:T(8,128)S(1)}, f32[3,64,256]{2,1,0:T(8,128)S(1)}, u32[]{:S(2)}, u32[]{:S(2)}) collective-permute-start(f32[3,64,256]{2,1,0:T(8,128)S(1)} %get-tuple-element.21), channel_id=1, source_target_pairs={{0,8},{8,0},{1,9},{9,1},{2,10},{10,2},{3,11},{11,3},{4,12},{12,4},... | collective-permute-start | bytes 589832 | tf_op jit(solution)/shard_map/ppermute | solution.py:271
  45.3 2.8 %shard_map.54 = (f32[32,1792]{1,0:T(8,128)S(1)}, f32[32,1792]{1,0:T(8,128)S(1)}, f32[32,1792]{1,0:T(8,128)S(1)}, f32[32,1792]{1,0:T(8,128)S(1)}) custom-call(s32[5]{0:T(128)S(1)} %stack.42.ids, f32[4,32,256]{2,1,0:T(8,128)S(1)} %collective-permute-done.4.refs_4_.b0, f32[4,32,256]{2,1,0:T(8,128)S(1)} %collective-permute-done.5.refs_5_.b1, ...), custom_call_target="tpu_custom_call" | custom-call | flops 1400000000 | bytes 5000000 | tf_op jit(solution)/shard_map/pallas_call | solution.py:157
  48.2 2.1 %collective-permute-start.18 = (f32[32,1792]{1,0:T(8,128)S(1)}, f32[32,1792]{1,0:T(8,128)S(1)}, u32[]{:S(2)}, u32[]{:S(2)}) collective-permute-start(f32[32,1792]{1,0:T(8,128)S(1)} %get-tuple-element.33), channel_id=1, source_target_pairs={{0,192},{64,0},{128,64},{192,128},{1,193},{65,1},{129,65},{193,129... | collective-permute-start | bytes 688136 | tf_op jit(solution)/shard_map/ppermute | solution.py:252
  52.1 2.3 %collective-permute-start.9 = (f32[64,256]{1,0:T(8,128)S(1)}, f32[64,256]{1,0:T(8,128)S(1)}, u32[]{:S(2)}, u32[]{:S(2)}) collective-permute-start(f32[64,256]{1,0:T(8,128)S(1)} %get-tuple-element.41), channel_id=1, source_target_pairs={{8,16},{24,32},{16,8},{40,48},{32,24},{56,64},{48,40},{72,80},{64,... | collective-permute-start | bytes 196616 | tf_op jit(solution)/shard_map/ppermute | solution.py:272
  55.6 3.1 %collective-permute-done.17 = f32[32,1792]{1,0:T(8,128)S(1)} collective-permute-done((f32[32,1792]{1,0:T(8,128)S(1)}, f32[32,1792]{1,0:T(8,128)S(1)}, u32[]{:S(2)}, u32[]{:S(2)}) %collective-permute-start.17) | collective-permute-done | bytes 229408 | tf_op jit(solution)/shard_map/ppermute | solution.py:252
  58.7 5.5 %collective-permute-done.16 = f32[32,1792]{1,0:T(8,128)S(1)} collective-permute-done((f32[32,1792]{1,0:T(8,128)S(1)}, f32[32,1792]{1,0:T(8,128)S(1)}, u32[]{:S(2)}, u32[]{:S(2)}) %collective-permute-start.16) | collective-permute-done | bytes 229408 | tf_op jit(solution)/shard_map/ppermute | solution.py:252
  64.4 1.5 %collective-permute-start.21 = (f32[16,1792]{1,0:T(8,128)S(1)}, f32[16,1792]{1,0:T(8,128)S(1)}, u32[]{:S(2)}, u32[]{:S(2)}) collective-permute-start(f32[16,1792]{1,0:T(8,128)S(1)} %get-tuple-element.39), channel_id=1, source_target_pairs={{0,48},{16,0},{32,16},{48,32},{1,49},{17,1},{33,17},{49,33},{2,50}... | collective-permute-start | bytes 344072 | tf_op jit(solution)/shard_map/ppermute | solution.py:267
  67.0 1.6 %collective-permute-done.21 = f32[16,1792]{1,0:T(8,128)S(1)} collective-permute-done((f32[16,1792]{1,0:T(8,128)S(1)}, f32[16,1792]{1,0:T(8,128)S(1)}, u32[]{:S(2)}, u32[]{:S(2)}) %collective-permute-start.21) | collective-permute-done | bytes 114720 | tf_op jit(solution)/shard_map/ppermute | solution.py:267
  68.7 7.8 %collective-permute-done.20 = f32[16,1792]{1,0:T(8,128)S(1)} collective-permute-done((f32[16,1792]{1,0:T(8,128)S(1)}, f32[16,1792]{1,0:T(8,128)S(1)}, u32[]{:S(2)}, u32[]{:S(2)}) %collective-permute-start.20) | collective-permute-done | bytes 114720 | tf_op jit(solution)/shard_map/ppermute | solution.py:267
  (47 shorter events, 7.8 us)
Async XLA Ops:
  1.5 6.6 %collective-permute-start = (f32[2,32,256]{2,1,0:T(8,128)S(1)}, f32[2,32,256]{2,1,0:T(8,128)S(1)}, u32[]{:S(2)}, u32[]{:S(2)}) collective-permute-start(f32[2,32,256]{2,1,0:T(8,128)S(1)} %bitcast.69), channel_id=1, source_target_pairs={{0,8},{8,0},{1,9},{9,1},{2,10},{10,2},{3,11},{11,3},{4,12},{12,4},... | collective-permute-start | bytes 196616 | tf_op jit(solution)/shard_map/ppermute | solution.py:226
  5.8 13.3 %collective-permute-start.10 = (f32[2,64,256]{2,1,0:T(8,128)S(1)}, f32[2,64,256]{2,1,0:T(8,128)S(1)}, u32[]{:S(2)}, u32[]{:S(2)}) collective-permute-start(f32[2,64,256]{2,1,0:T(8,128)S(1)} %get-tuple-element.23.own), channel_id=1, source_target_pairs={{0,8},{8,0},{1,9},{9,1},{2,10},{10,2},{3,11},{11,3},{4,12},{12,4},... | collective-permute-start | bytes 393224 | tf_op jit(solution)/shard_map/ppermute | solution.py:242
  5.9 12.0 %collective-permute-start.11 = (f32[64,256]{1,0:T(8,128)S(1)}, f32[64,256]{1,0:T(8,128)S(1)}, u32[]{:S(2)}, u32[]{:S(2)}) collective-permute-start(f32[64,256]{1,0:T(8,128)S(1)} %dynamic-slice_bitcast_fusion.3), channel_id=1, source_target_pairs={{8,16},{24,32},{16,8},{40,48},{32,24},{56,64},{48,40},{72,80},{64,... | collective-permute-start | bytes 196616 | tf_op jit(solution)/shard_map/ppermute | solution.py:243
  8.2 17.3 %collective-permute-start.4 = (f32[4,32,256]{2,1,0:T(8,128)S(1)}, f32[4,32,256]{2,1,0:T(8,128)S(1)}, u32[]{:S(2)}, u32[]{:S(2)}) collective-permute-start(f32[4,32,256]{2,1,0:T(8,128)S(1)} %pad_maximum_fusion.1.refs_0_.b0), channel_id=1, source_target_pairs={{0,1},{1,0},{2,3},{3,2},{4,5},{5,4},{6,7},{7,6},{8,9},{9,8},{10,11... | collective-permute-start | bytes 393224 | tf_op jit(solution)/shard_map/ppermute | solution.py:227
  14.3 12.8 %collective-permute-start.1 = (f32[4,32,256]{2,1,0:T(8,128)S(1)}, f32[4,32,256]{2,1,0:T(8,128)S(1)}, u32[]{:S(2)}, u32[]{:S(2)}) collective-permute-start(f32[4,32,256]{2,1,0:T(8,128)S(1)} %pad_maximum_fusion.1.refs_0_.b0), channel_id=1, source_target_pairs={{0,2},{2,4},{4,6},{6,0},{1,3},{3,5},{5,7},{7,1},{8,10},{10,12},{12... | collective-permute-start | bytes 393224 | tf_op jit(solution)/shard_map/ppermute | solution.py:228
  15.5 12.9 %collective-permute-start.2 = (f32[4,32,256]{2,1,0:T(8,128)S(1)}, f32[4,32,256]{2,1,0:T(8,128)S(1)}, u32[]{:S(2)}, u32[]{:S(2)}) collective-permute-start(f32[4,32,256]{2,1,0:T(8,128)S(1)} %pad_maximum_fusion.1.refs_0_.b0), channel_id=1, source_target_pairs={{0,4},{2,6},{4,0},{6,2},{1,5},{3,7},{5,1},{7,3},{8,12},{10,14},{12... | collective-permute-start | bytes 393224 | tf_op jit(solution)/shard_map/ppermute | solution.py:228
  17.9 10.4 %collective-permute-start.3 = (f32[4,32,256]{2,1,0:T(8,128)S(1)}, f32[4,32,256]{2,1,0:T(8,128)S(1)}, u32[]{:S(2)}, u32[]{:S(2)}) collective-permute-start(f32[4,32,256]{2,1,0:T(8,128)S(1)} %pad_maximum_fusion.1.refs_0_.b0), channel_id=1, source_target_pairs={{0,6},{2,0},{4,2},{6,4},{1,7},{3,1},{5,3},{7,5},{8,14},{10,8},{12,... | collective-permute-start | bytes 393224 | tf_op jit(solution)/shard_map/ppermute | solution.py:228
  19.1 4.2 %collective-permute-start.12 = (f32[64,256]{1,0:T(8,128)S(1)}, f32[64,256]{1,0:T(8,128)S(1)}, u32[]{:S(2)}, u32[]{:S(2)}) collective-permute-start(f32[64,256]{1,0:T(8,128)S(1)} %collective-permute-done.11.edge), channel_id=1, source_target_pairs={{0,8},{8,0},{1,9},{9,1},{2,10},{10,2},{3,11},{11,3},{4,12},{12,4},... | collective-permute-start | bytes 196616 | tf_op jit(solution)/shard_map/ppermute | solution.py:244
  19.2 2.0 %copy-start = (f32[27,64,512]{2,1,0:T(8,128)S(1)}, f32[27,64,512]{2,1,0:T(8,128)}, u32[]{:S(2)}) copy-start(f32[27,64,512]{2,1,0:T(8,128)} %w_ref.1) | copy-start | bytes 10616836
  25.5 10.8 %collective-permute-start.5 = (f32[4,32,256]{2,1,0:T(8,128)S(1)}, f32[4,32,256]{2,1,0:T(8,128)S(1)}, u32[]{:S(2)}, u32[]{:S(2)}) collective-permute-start(f32[4,32,256]{2,1,0:T(8,128)S(1)} %collective-permute-done.4.refs_4_.b0), channel_id=1, source_target_pairs={{0,2},{2,4},{4,6},{6,0},{1,3},{3,5},{5,7},{7,1},{8,10},{10,12},{12... | collective-permute-start | bytes 393224 | tf_op jit(solution)/shard_map/ppermute | solution.py:229
  25.8 12.0 %collective-permute-start.6 = (f32[4,32,256]{2,1,0:T(8,128)S(1)}, f32[4,32,256]{2,1,0:T(8,128)S(1)}, u32[]{:S(2)}, u32[]{:S(2)}) collective-permute-start(f32[4,32,256]{2,1,0:T(8,128)S(1)} %collective-permute-done.4.refs_4_.b0), channel_id=1, source_target_pairs={{0,4},{2,6},{4,0},{6,2},{1,5},{3,7},{5,1},{7,3},{8,12},{10,14},{12... | collective-permute-start | bytes 393224 | tf_op jit(solution)/shard_map/ppermute | solution.py:229
  27.0 10.8 %collective-permute-start.7 = (f32[4,32,256]{2,1,0:T(8,128)S(1)}, f32[4,32,256]{2,1,0:T(8,128)S(1)}, u32[]{:S(2)}, u32[]{:S(2)}) collective-permute-start(f32[4,32,256]{2,1,0:T(8,128)S(1)} %collective-permute-done.4.refs_4_.b0), channel_id=1, source_target_pairs={{0,6},{2,0},{4,2},{6,4},{1,7},{3,1},{5,3},{7,5},{8,14},{10,8},{12,... | collective-permute-start | bytes 393224 | tf_op jit(solution)/shard_map/ppermute | solution.py:229
  31.2 19.1 %collective-permute-start.15 = (f32[32,1792]{1,0:T(8,128)S(1)}, f32[32,1792]{1,0:T(8,128)S(1)}, u32[]{:S(2)}, u32[]{:S(2)}) collective-permute-start(f32[32,1792]{1,0:T(8,128)S(1)} %get-tuple-element.29), channel_id=1, source_target_pairs={{0,192},{64,0},{128,64},{192,128},{1,193},{65,1},{129,65},{193,129... | collective-permute-start | bytes 688136 | tf_op jit(solution)/shard_map/ppermute | solution.py:252
  36.2 15.1 %collective-permute-start.14 = (f32[32,1792]{1,0:T(8,128)S(1)}, f32[32,1792]{1,0:T(8,128)S(1)}, u32[]{:S(2)}, u32[]{:S(2)}) collective-permute-start(f32[32,1792]{1,0:T(8,128)S(1)} %get-tuple-element.28), channel_id=1, source_target_pairs={{0,128},{64,192},{128,0},{192,64},{1,129},{65,193},{129,1},{193,65... | collective-permute-start | bytes 688136 | tf_op jit(solution)/shard_map/ppermute | solution.py:252
  36.3 15.7 %collective-permute-start.13 = (f32[32,1792]{1,0:T(8,128)S(1)}, f32[32,1792]{1,0:T(8,128)S(1)}, u32[]{:S(2)}, u32[]{:S(2)}) collective-permute-start(f32[32,1792]{1,0:T(8,128)S(1)} %get-tuple-element.27), channel_id=1, source_target_pairs={{0,64},{64,128},{128,192},{192,0},{1,65},{65,129},{129,193},{193,1... | collective-permute-start | bytes 688136 | tf_op jit(solution)/shard_map/ppermute | solution.py:252
  44.1 8.0 %collective-permute-start.8 = (f32[3,64,256]{2,1,0:T(8,128)S(1)}, f32[3,64,256]{2,1,0:T(8,128)S(1)}, u32[]{:S(2)}, u32[]{:S(2)}) collective-permute-start(f32[3,64,256]{2,1,0:T(8,128)S(1)} %get-tuple-element.21), channel_id=1, source_target_pairs={{0,8},{8,0},{1,9},{9,1},{2,10},{10,2},{3,11},{11,3},{4,12},{12,4},... | collective-permute-start | bytes 589832 | tf_op jit(solution)/shard_map/ppermute | solution.py:271
  48.2 7.4 %collective-permute-start.18 = (f32[32,1792]{1,0:T(8,128)S(1)}, f32[32,1792]{1,0:T(8,128)S(1)}, u32[]{:S(2)}, u32[]{:S(2)}) collective-permute-start(f32[32,1792]{1,0:T(8,128)S(1)} %get-tuple-element.33), channel_id=1, source_target_pairs={{0,192},{64,0},{128,64},{192,128},{1,193},{65,1},{129,65},{193,129... | collective-permute-start | bytes 688136 | tf_op jit(solution)/shard_map/ppermute | solution.py:252
  50.3 8.4 %collective-permute-start.17 = (f32[32,1792]{1,0:T(8,128)S(1)}, f32[32,1792]{1,0:T(8,128)S(1)}, u32[]{:S(2)}, u32[]{:S(2)}) collective-permute-start(f32[32,1792]{1,0:T(8,128)S(1)} %get-tuple-element.32), channel_id=1, source_target_pairs={{0,128},{64,192},{128,0},{192,64},{1,129},{65,193},{129,1},{193,65... | collective-permute-start | bytes 688136 | tf_op jit(solution)/shard_map/ppermute | solution.py:252
  51.3 12.9 %collective-permute-start.16 = (f32[32,1792]{1,0:T(8,128)S(1)}, f32[32,1792]{1,0:T(8,128)S(1)}, u32[]{:S(2)}, u32[]{:S(2)}) collective-permute-start(f32[32,1792]{1,0:T(8,128)S(1)} %get-tuple-element.31), channel_id=1, source_target_pairs={{0,64},{64,128},{128,192},{192,0},{1,65},{65,129},{129,193},{193,1... | collective-permute-start | bytes 688136 | tf_op jit(solution)/shard_map/ppermute | solution.py:252
  52.1 14.1 %collective-permute-start.9 = (f32[64,256]{1,0:T(8,128)S(1)}, f32[64,256]{1,0:T(8,128)S(1)}, u32[]{:S(2)}, u32[]{:S(2)}) collective-permute-start(f32[64,256]{1,0:T(8,128)S(1)} %get-tuple-element.41), channel_id=1, source_target_pairs={{8,16},{24,32},{16,8},{40,48},{32,24},{56,64},{48,40},{72,80},{64,... | collective-permute-start | bytes 196616 | tf_op jit(solution)/shard_map/ppermute | solution.py:272
  64.4 4.3 %collective-permute-start.21 = (f32[16,1792]{1,0:T(8,128)S(1)}, f32[16,1792]{1,0:T(8,128)S(1)}, u32[]{:S(2)}, u32[]{:S(2)}) collective-permute-start(f32[16,1792]{1,0:T(8,128)S(1)} %get-tuple-element.39), channel_id=1, source_target_pairs={{0,48},{16,0},{32,16},{48,32},{1,49},{17,1},{33,17},{49,33},{2,50}... | collective-permute-start | bytes 344072 | tf_op jit(solution)/shard_map/ppermute | solution.py:267
  65.9 10.6 %collective-permute-start.20 = (f32[16,1792]{1,0:T(8,128)S(1)}, f32[16,1792]{1,0:T(8,128)S(1)}, u32[]{:S(2)}, u32[]{:S(2)}) collective-permute-start(f32[16,1792]{1,0:T(8,128)S(1)} %get-tuple-element.40), channel_id=1, source_target_pairs={{0,32},{16,48},{32,0},{48,16},{1,33},{17,49},{33,1},{49,17},{2,34}... | collective-permute-start | bytes 344072 | tf_op jit(solution)/shard_map/ppermute | solution.py:267
  65.9 10.6 %collective-permute-start.19 = (f32[16,1792]{1,0:T(8,128)S(1)}, f32[16,1792]{1,0:T(8,128)S(1)}, u32[]{:S(2)}, u32[]{:S(2)}) collective-permute-start(f32[16,1792]{1,0:T(8,128)S(1)} %get-tuple-element.38), channel_id=1, source_target_pairs={{0,16},{16,32},{32,48},{48,0},{1,17},{17,33},{33,49},{49,1},{2,18}... | collective-permute-start | bytes 344072 | tf_op jit(solution)/shard_map/ppermute | solution.py:267

commit v2 on v1

v2 whole, which is shorter than its diff:
```python
import math

import jax
import jax.numpy as jnp
from jax import lax
from jax.experimental import pallas as pl
from jax.experimental.pallas import tpu as pltpu
from jax.sharding import Mesh, PartitionSpec as P


W = 16
CELLS = 256
TAPS = 576
LANES = 1792
GRANT = 24 * 1024 * 1024
DEPTH_AXES = ("y", "zl", "core")
NT = (((1,), (1,)), ((), ()))
NN = (((1,), (0,)), ((), ()))


def normal_cdf(value):
    return 0.5 * (1.0 + jax.scipy.special.erf(value / math.sqrt(2.0)))


def split(value):
    hi = value.astype(jnp.bfloat16)
    lo = (value - hi.astype(jnp.float32)).astype(jnp.bfloat16)
    return hi, lo


def mul(a, b, dims):
    return lax.dot_general(a, b, dims, preferred_element_type=jnp.float32)


def moved(block, step):
    return block if step == 0 else pltpu.roll(block, (-step) % CELLS, 1)


def col_ok(shape, dcol):
    column = lax.broadcasted_iota(jnp.int32, shape, 1) % W
    return (column + dcol >= 0) & (column + dcol < W)


def row_ok(shape, drow):
    row = lax.broadcasted_iota(jnp.int32, shape, 1) // W
    return (row + drow >= 0) & (row + drow < CELLS // W)


def shift_cols(block, dcol):
    if dcol == 0:
        return block
    return jnp.where(col_ok(block.shape, dcol), moved(block, dcol), 0.0)


def shift_rows(block, drow):
    if drow == 0:
        return block
    return jnp.where(row_ok(block.shape, drow), moved(block, drow * W), 0.0)


def call(kernel, out_shapes, n_in, scratch=(), flops=0, moved_bytes=0):
    vmem = pl.BlockSpec(memory_space=pltpu.VMEM)
    return pl.pallas_call(
        kernel,
        out_shape=out_shapes,
        in_specs=[pl.BlockSpec(memory_space=pltpu.SMEM)] + [vmem] * n_in,
        out_specs=jax.tree.map(lambda _: vmem, out_shapes),
        scratch_shapes=scratch,
        cost_estimate=pl.CostEstimate(flops=flops, bytes_accessed=moved_bytes, transcendentals=0),
        compiler_params=pltpu.CompilerParams(vmem_limit_bytes=GRANT),
    )


def weight_kernel(ids, w_ref, out_ref):
    place = 2 * ids[1] + ids[2]
    group = (lax.broadcasted_iota(jnp.int32, (64, 128), 1) // 16) % 4

    def tap_body(tap, carry):
        rows = pl.ds(pl.multiple_of(64 * tap, 64), 64)
        for kd in range(3):
            picked = jnp.zeros((64, 128), jnp.float32)
            for src in range(4):
                lanes = w_ref[9 * kd + tap, :, 128 * src : 128 * src + 128]
                turned = pltpu.roll(lanes, (16 * (src - place) + 128) % 128, 1)
                picked = jnp.where(group == src, turned, picked)
            hi, lo = split(picked)
            out_ref[rows, 128 * kd : 128 * kd + 128] = hi
            out_ref[rows, 384 + 128 * kd : 384 + 128 * kd + 128] = lo
        return carry

    lax.fori_loop(0, 9, tap_body, 0)


def pick_weights(ids, weight):
    shape = jax.ShapeDtypeStruct((TAPS, 768), jnp.bfloat16)
    return call(weight_kernel, shape, 1, flops=200000000, moved_bytes=5000000)(ids, weight)


def act_kernel(ids, own, sib, pair, cross, before, after, hi_ref, lo_ref):
    base = 4 * ids[1] + 2 * ids[2]
    planes = [(before[...], 0), (after[...], 9)]
    for n, block in enumerate((own, sib, pair, cross)):
        planes += [(block[j], (base ^ (2 * n)) + 1 + j) for j in range(2)]
    for block, place in planes:
        for dcol in (-1, 0, 1):
            cols = shift_cols(block, dcol)
            for drow in (-1, 0, 1):
                hi, lo = split(shift_rows(cols, drow))
                tap = 3 * (drow + 1) + dcol + 1
                rows = pl.ds(pl.multiple_of(TAPS * place + 64 * tap, 64), 64)
                hi_ref[rows, :] = hi
                lo_ref[rows, :] = lo
    hi_ref[10 * TAPS :, :] = jnp.zeros((64, CELLS), jnp.bfloat16)
    lo_ref[10 * TAPS :, :] = jnp.zeros((64, CELLS), jnp.bfloat16)


def expand_act(ids, *planes):
    shape = jax.ShapeDtypeStruct((10 * TAPS + 64, CELLS), jnp.bfloat16)
    return call(act_kernel, (shape, shape), 6, flops=50000000, moved_bytes=4000000)(ids, *planes)


def filter_kernel(ids, *refs):
    blocks, (ahi, alo), outs, both = refs[:8], refs[8:10], refs[10:14], refs[14]
    y, x, base = ids[0], ids[3], 4 * ids[1] + 2 * ids[2]
    for n, block in enumerate(blocks):
        u = (x - n % 4 - y + 8) % 4
        row = 32 * u + 16 * (n // 4)
        for i in range(4):
            for j in range(2):
                q = (base ^ (2 * i)) + j
                hi, lo = split(block[2 * i + j])
                both[q, pl.ds(pl.multiple_of(row, 16), 16), :] = hi
                both[q, pl.ds(pl.multiple_of(row + 128, 16), 16), :] = lo
    for n in range(LANES // 256):
        wide = jnp.zeros((256, 256), jnp.float32)
        narrow = jnp.zeros((128, 256), jnp.float32)
        for q in range(8):
            taps = slice(TAPS * q + 256 * n, TAPS * q + 256 * n + 256)
            wide += mul(both[q], ahi[taps, :], NT)
            narrow += mul(both[q, :128], alo[taps, :], NT)
        total = wide[:128] + wide[128:] + narrow
        for u in range(4):
            outs[u][:, 256 * n : 256 * n + 256] = total[32 * u : 32 * u + 32]


def filter_terms(ids, blocks, ahi, alo):
    shape = jax.ShapeDtypeStruct((32, LANES), jnp.float32)
    scratch = [pltpu.VMEM((8, 256, CELLS), jnp.bfloat16)]
    return call(
        filter_kernel, (shape,) * 4, 10, scratch, flops=2800000000, moved_bytes=9000000
    )(ids, *blocks, ahi, alo)


KEPT = (0, 1, 2, 5, 6)


def grad_kernel(ids, *refs):
    blocks, (w_ref, keep, send, ghi, glo) = refs[:8], refs[8:]
    core, x, zh, base = ids[2], ids[3], ids[4], 4 * ids[1] + 2 * ids[2]
    for n, block in enumerate(blocks):
        src_x = (x - n % 4 + 4) % 4
        src_zh = zh if n < 4 else 1 - zh
        place = 64 * src_zh + 16 * src_x
        for i in range(4):
            for j in range(2):
                q = (base ^ (2 * i)) + j
                hi, lo = split(block[2 * i + j])
                rows = pl.ds(pl.multiple_of((7 - q) * 128 + place, 16), 16)
                ghi[rows, :] = hi
                glo[rows, :] = lo
    for p in range(10):
        first, last = max(0, p - 7), min(2, p)
        whi = w_ref[:, 128 * first : 128 * (last + 1)]
        wlo = w_ref[:, 384 + 128 * first : 384 + 128 * (last + 1)]
        top = 128 * (7 - p + first)
        depth = slice(top, top + 128 * (last + 1 - first))
        z = mul(
            jnp.concatenate([whi, wlo, whi], axis=1),
            jnp.concatenate([ghi[depth, :], ghi[depth, :], glo[depth, :]], axis=0),
            NN,
        )
        total = None
        for kh in range(3):
            rows = z[192 * kh : 192 * kh + 192]
            part = shift_cols(rows[:64], 1) + rows[64:128] + shift_cols(rows[128:], -1)
            part = shift_rows(part, 1 - kh)
            total = part if total is None else total + part
        kept_by_first = p in KEPT
        m = KEPT.index(p if kept_by_first else 9 - p)
        mine = core == (0 if kept_by_first else 1)

        @pl.when(mine)
        def _():
            keep[m] = total

        @pl.when(jnp.logical_not(mine))
        def _():
            send[m] = total


def grad_terms(ids, blocks, weights):
    shape = jax.ShapeDtypeStruct((5, 64, CELLS), jnp.float32)
    scratch = [pltpu.VMEM((8 * 128, CELLS), jnp.bfloat16)] * 2
    return call(
        grad_kernel, (shape, shape), 9, scratch, flops=2800000000, moved_bytes=4000000
    )(ids, *blocks, weights)


def ring(n, step):
    return [(i, (i + step) % n) for i in range(n)]


def sent(x, axis, pairs):
    return lax.ppermute(x, axis, pairs)


def pick(x, index, axis=0):
    return lax.dynamic_index_in_dim(x, index, axis, keepdims=False)


def work(pre, grad_out, weight):
    y, zl, core, x, zh = [lax.axis_index(a) for a in ("y", "zl", "core", "x", "zh")]
    side, half = zl % 2, zl // 2
    ids = jnp.stack([y, side, core, x, zh]).astype(jnp.int32)
    swap = [(0, 1), (1, 0)]
    pair_swap = [(i, i ^ 1) for i in range(4)]
    half_swap = [(i, i ^ 2) for i in range(4)]
    outward = [(4 * n + 3, 4 * n + 4) for n in range(7)] + [(4 * n + 4, 4 * n + 3) for n in range(7)]

    cot = jnp.moveaxis(grad_out[0], 1, 0).reshape(2, 2, 2, 16, CELLS)
    theirs = sent(pick(cot, 1 - core, 2), "core", swap)
    chip = jnp.stack([pick(cot, core, 2), theirs]).reshape(4, 2, 16, CELLS)
    theirs = sent(pick(chip, 1 - side, 1), "zl", pair_swap)
    cot8 = jnp.concatenate([pick(chip, side, 1), theirs], axis=0)
    across = sent(cot8, "zh", swap)
    blocks = [cot8] + [sent(cot8, "x", ring(4, s)) for s in (1, 2, 3)]
    blocks += [across] + [sent(across, "x", ring(4, s)) for s in (1, 2, 3)]

    source = jnp.moveaxis(pre[0], 1, 0)
    cdf = normal_cdf(source)
    slope = cdf + source * jnp.exp(-0.5 * source * source) / math.sqrt(2.0 * math.pi)
    own, slope = lax.optimization_barrier((source * cdf, slope))
    pair = sent(own, "zl", pair_swap)
    sib = sent(own, "core", swap)
    cross = sent(pair, "core", swap)
    place = 2 * side + core
    top = jnp.where(
        place < 2,
        jnp.where(place == 0, cross[1], pair[1]),
        jnp.where(place == 2, sib[1], own[1]),
    )
    bottom = jnp.where(
        place < 2,
        jnp.where(place == 0, own[0], sib[0]),
        jnp.where(place == 2, pair[0], cross[0]),
    )
    before = sent(top, DEPTH_AXES, [(d, d + 4) for d in range(28)])
    after = sent(bottom, DEPTH_AXES, [(d + 4, d) for d in range(28)])

    weights = pick_weights(ids, weight)
    ahi, alo = expand_act(ids, own, sib, pair, cross, before, after)

    parts = filter_terms(ids, blocks, ahi, alo)
    total = parts[0]
    for t in (1, 2, 3):
        total = total + sent(parts[t], "y", ring(4, t))
    total = total.reshape(2, 16, LANES)
    kept = pick(total, (half + zh) % 2)
    total = kept + sent(pick(total, (half + zh + 1) % 2), "zl", half_swap)
    total = total * float(16384) ** (-0.5)
    grad_weight = total.reshape(16, 28, 64)[:, :27].transpose(1, 2, 0)

    keep, send = grad_terms(ids, blocks, weights)
    got = keep + sent(send, "core", swap)
    outer, inner = got[:3], jnp.concatenate([got[:1], got[3:]], axis=0)
    edge = side == core
    got = jnp.where(edge, outer, inner) + sent(jnp.where(edge, inner, outer), "zl", pair_swap)
    close = got[1] + sent(got[0], DEPTH_AXES, outward)
    grad_act = jnp.where(core == 0, jnp.stack([close, got[2]]), jnp.stack([got[2], close]))
    grad_pre = jnp.moveaxis(grad_act * slope, 0, 1)[None]
    return (grad_pre, grad_weight)


def solution(mesh):
    fine = Mesh(mesh.devices.reshape(4, 4, 2, 4, 2), ("y", "zl", "core", "x", "zh"))
    chan, depth = ("x", "zh"), DEPTH_AXES
    return jax.shard_map(
        work,
        mesh=fine,
        in_specs=(P(None, chan, depth, None), P(None, chan, depth, None), P(None, chan, None)),
        out_specs=(P(None, chan, depth, None), P(None, chan, depth)),
        check_vma=False,
    )
```

time: 77.7 us -> 80.9 us (1.041)
  the two profiles are of different devices: /device:TPU:1 before, /device:TPU:8 now
where the time goes in v2:
time: 80.9 us; the launch traced here: 80.7 us
  starting transfers between devices  36.8 us (45%)
  Pallas kernels  20.1 us (25%)
  waiting for transfers between devices  16.9 us (21%)
  local copies, waits for them, and re-layouts  4.78 us (6%)
  other arithmetic  1.22 us (2%)
  between operations  0.89 us (1%)
    ppermute x21, starting transfers between devices, sent(): return lax.ppermute(x, axis, pairs)  36.8 us
    ppermute x21, waiting for transfers between devices, sent(): return lax.ppermute(x, axis, pairs)  16.9 us
    pallas_call x1, Pallas kernels, grad_terms(): call(grad_kernel, (shape, shape), 9, scratch, flops=2800000000, moved_byt...  9.75 us
    pallas_call x1, Pallas kernels, filter_terms(): call(filter_kernel, (shape,) * 4, 10, scratch, flops=2800000000, moved_by...  5.04 us
    unnamed x5, local copies, waits for them, and re-layouts  4.49 us
    pallas_call x1, Pallas kernels, expand_act(): call(act_kernel, (shape, shape), 6, flops=50000000, moved_bytes=4000000)  3.16 us
    pallas_call x1, Pallas kernels, pick_weights(): call(weight_kernel, shape, 1, flops=200000000, moved_bytes=5000000)  2.12 us
  transfers between devices with their start and end apart: 21, of which 7 were waited for; matrix products, arithmetic and copies ran while one was open for 3% of the time, Pallas kernels for 19%

profile of v2, /device:TPU:8, one launch (start us, length us, event | category | flops | bytes accessed | tf_op | source)
XLA Modules:
  0.0 80.7 jit_solution(12096354153758569730)
XLA Ops:
  1.7 1.0 %fusion.3 = (f32[2,64,256]{2,1,0:T(8,128)S(1)}, f32[2,64,256]{2,1,0:T(8,128)S(1)}) fusion(f32[1,64,2,256]{3,2,1,0:T(2,128)} %param.3), kind=kLoop, calls=%fused_computation.9 | loop fusion | flops 294912 | bytes 393216 | tf_op jit(solution)/shard_map/add | solution.py:241
  2.6 2.0 %collective-permute-start.13 = (f32[2,64,256]{2,1,0:T(8,128)S(1)}, f32[2,64,256]{2,1,0:T(8,128)S(1)}, u32[]{:S(2)}, u32[]{:S(2)}) collective-permute-start(f32[2,64,256]{2,1,0:T(8,128)S(1)} %get-tuple-element.15.own), channel_id=1, source_target_pairs={{0,16},{16,0},{32,48},{48,32},{1,17},{17,1},{33,49},{49,33},{2,18}... | collective-permute-start | bytes 393224 | tf_op jit(solution)/shard_map/ppermute | solution.py:214
  5.1 4.0 %collective-permute-done.13.pair = f32[2,64,256]{2,1,0:T(8,128)S(1)} collective-permute-done((f32[2,64,256]{2,1,0:T(8,128)S(1)}, f32[2,64,256]{2,1,0:T(8,128)S(1)}, u32[]{:S(2)}, u32[]{:S(2)}) %collective-permute-start.13) | collective-permute-done | bytes 131104 | tf_op jit(solution)/shard_map/ppermute | solution.py:214
  9.1 1.1 %collective-permute-done.1 = f32[4,16,256]{2,1,0:T(8,128)S(1)} collective-permute-done((f32[4,16,256]{2,1,0:T(8,128)S(1)}, f32[4,16,256]{2,1,0:T(8,128)S(1)}, u32[]{:S(2)}, u32[]{:S(2)}) %collective-permute-start.1) | collective-permute-done | bytes 65568 | tf_op jit(solution)/shard_map/ppermute | solution.py:214
  10.2 7.1 %collective-permute-start.5 = (f32[8,16,256]{2,1,0:T(8,128)S(1)}, f32[8,16,256]{2,1,0:T(8,128)S(1)}, u32[]{:S(2)}, u32[]{:S(2)}) collective-permute-start(f32[8,16,256]{2,1,0:T(8,128)S(1)} %pad_maximum_fusion.2.refs_0_), channel_id=1, source_target_pairs={{0,1},{1,0},{2,3},{3,2},{4,5},{5,4},{6,7},{7,6},{8,9},{9,8},{10,11... | collective-permute-start | bytes 393224 | tf_op jit(solution)/shard_map/ppermute | solution.py:214
  17.3 2.8 %collective-permute-start.4 = (f32[8,16,256]{2,1,0:T(8,128)S(1)}, f32[8,16,256]{2,1,0:T(8,128)S(1)}, u32[]{:S(2)}, u32[]{:S(2)}) collective-permute-start(f32[8,16,256]{2,1,0:T(8,128)S(1)} %pad_maximum_fusion.2.refs_0_), channel_id=1, source_target_pairs={{0,6},{2,0},{4,2},{6,4},{1,7},{3,1},{5,3},{7,5},{8,14},{10,8},{12,... | collective-permute-start | bytes 393224 | tf_op jit(solution)/shard_map/ppermute | solution.py:214
  20.1 3.3 %collective-permute-start.16 = (f32[64,256]{1,0:T(8,128)S(1)}, f32[64,256]{1,0:T(8,128)S(1)}, u32[]{:S(2)}, u32[]{:S(2)}) collective-permute-start(f32[64,256]{1,0:T(8,128)S(1)} %get-tuple-element.28), channel_id=1, source_target_pairs={{32,0},{40,8},{48,16},{56,24},{64,32},{72,40},{80,48},{88,56},{96,... | collective-permute-start | bytes 196616 | tf_op jit(solution)/shard_map/ppermute | solution.py:214
  23.4 3.5 %collective-permute-start.15 = (f32[64,256]{1,0:T(8,128)S(1)}, f32[64,256]{1,0:T(8,128)S(1)}, u32[]{:S(2)}, u32[]{:S(2)}) collective-permute-start(f32[64,256]{1,0:T(8,128)S(1)} %get-tuple-element.29), channel_id=1, source_target_pairs={{0,32},{8,40},{16,48},{24,56},{32,64},{40,72},{48,80},{56,88},{64,... | collective-permute-start | bytes 196616 | tf_op jit(solution)/shard_map/ppermute | solution.py:214
  28.7 2.4 %collective-permute-start.8 = (f32[8,16,256]{2,1,0:T(8,128)S(1)}, f32[8,16,256]{2,1,0:T(8,128)S(1)}, u32[]{:S(2)}, u32[]{:S(2)}) collective-permute-start(f32[8,16,256]{2,1,0:T(8,128)S(1)} %collective-permute-done.5.refs_4_), channel_id=1, source_target_pairs={{0,6},{2,0},{4,2},{6,4},{1,7},{3,1},{5,3},{7,5},{8,14},{10,8},{12,... | collective-permute-start | bytes 393224 | tf_op jit(solution)/shard_map/ppermute | solution.py:214
  31.0 1.5 %collective-permute-start.7 = (f32[8,16,256]{2,1,0:T(8,128)S(1)}, f32[8,16,256]{2,1,0:T(8,128)S(1)}, u32[]{:S(2)}, u32[]{:S(2)}) collective-permute-start(f32[8,16,256]{2,1,0:T(8,128)S(1)} %collective-permute-done.5.refs_4_), channel_id=1, source_target_pairs={{0,4},{2,6},{4,0},{6,2},{1,5},{3,7},{5,1},{7,3},{8,12},{10,14},{12... | collective-permute-start | bytes 393224 | tf_op jit(solution)/shard_map/ppermute | solution.py:214
  32.6 2.0 %copy-done = f32[27,64,512]{2,1,0:T(8,128)S(1)} copy-done((f32[27,64,512]{2,1,0:T(8,128)S(1)}, f32[27,64,512]{2,1,0:T(8,128)}, u32[]{:S(2)}) %copy-start) | copy-done | bytes 3538968
  34.6 2.1 %shard_map.50.refs_8_ = bf16[576,768]{1,0:T(8,128)(2,1)S(1)} custom-call(s32[5]{0:T(128)S(1)} %stack.42.ids, f32[27,64,512]{2,1,0:T(8,128)S(1)} %copy-done), custom_call_target="tpu_custom_call" | custom-call | flops 200000000 | bytes 5000000 | tf_op jit(solution)/shard_map/pallas_call | solution.py:96
  36.8 3.2 %shard_map.52 = (bf16[5824,256]{1,0:T(8,128)(2,1)S(1)}, bf16[5824,256]{1,0:T(8,128)(2,1)S(1)}) custom-call(s32[5]{0:T(128)S(1)} %stack.42.ids, f32[2,64,256]{2,1,0:T(8,128)S(1)} %get-tuple-element.15.own, f32[2,64,256]{2,1,0:T(8,128)S(1)} %collective-permute-done.12.sib, f32[2,64,256]{2,1,0:T(8,128)S(1)} %collective-permute-done.13.pair, ...), custom_call_target="tpu_custom_call" | custom-call | flops 50000000 | bytes 4000000 | tf_op jit(solution)/shard_map/pallas_call | solution.py:119
  40.8 5.0 %shard_map.53 = (f32[32,1792]{1,0:T(8,128)S(1)}, f32[32,1792]{1,0:T(8,128)S(1)}, f32[32,1792]{1,0:T(8,128)S(1)}, f32[32,1792]{1,0:T(8,128)S(1)}) custom-call(s32[5]{0:T(128)S(1)} %stack.42.ids, f32[8,16,256]{2,1,0:T(8,128)S(1)} %pad_maximum_fusion.2.refs_0_, f32[8,16,256]{2,1,0:T(8,128)S(1)} %collective-permute-done.2.refs_1_, ...), custom_call_target="tpu_custom_call" | custom-call | flops 2800000000 | bytes 9000000 | tf_op jit(solution)/shard_map/pallas_call | solution.py:149
  45.9 1.6 %collective-permute-start.17 = (f32[32,1792]{1,0:T(8,128)S(1)}, f32[32,1792]{1,0:T(8,128)S(1)}, u32[]{:S(2)}, u32[]{:S(2)}) collective-permute-start(f32[32,1792]{1,0:T(8,128)S(1)} %get-tuple-element.19), channel_id=1, source_target_pairs={{0,64},{64,128},{128,192},{192,0},{1,65},{65,129},{129,193},{193,1... | collective-permute-start | bytes 688136 | tf_op jit(solution)/shard_map/ppermute | solution.py:214
  47.5 1.0 %collective-permute-start.18 = (f32[32,1792]{1,0:T(8,128)S(1)}, f32[32,1792]{1,0:T(8,128)S(1)}, u32[]{:S(2)}, u32[]{:S(2)}) collective-permute-start(f32[32,1792]{1,0:T(8,128)S(1)} %get-tuple-element.20), channel_id=1, source_target_pairs={{0,128},{64,192},{128,0},{192,64},{1,129},{65,193},{129,1},{193,65... | collective-permute-start | bytes 688136 | tf_op jit(solution)/shard_map/ppermute | solution.py:214
  48.5 2.4 %collective-permute-start.19 = (f32[32,1792]{1,0:T(8,128)S(1)}, f32[32,1792]{1,0:T(8,128)S(1)}, u32[]{:S(2)}, u32[]{:S(2)}) collective-permute-start(f32[32,1792]{1,0:T(8,128)S(1)} %get-tuple-element.21), channel_id=1, source_target_pairs={{0,192},{64,0},{128,64},{192,128},{1,193},{65,1},{129,65},{193,129... | collective-permute-start | bytes 688136 | tf_op jit(solution)/shard_map/ppermute | solution.py:214
  50.9 9.7 %shard_map.51 = (f32[5,64,256]{2,1,0:T(8,128)S(1)}, f32[5,64,256]{2,1,0:T(8,128)S(1)}) custom-call(s32[5]{0:T(128)S(1)} %stack.42.ids, f32[8,16,256]{2,1,0:T(8,128)S(1)} %pad_maximum_fusion.2.refs_0_, f32[8,16,256]{2,1,0:T(8,128)S(1)} %collective-permute-done.2.refs_1_, f32[8,16,256]{2,1,0:T(8,128)S(1)} %collective-permute-done.3.refs_2_, ...), custom_call_target="tpu_custom_call" | custom-call | flops 2800000000 | bytes 4000000 | tf_op jit(solution)/shard_map/pallas_call | solution.py:204
  60.8 1.3 %collective-permute-start.20 = (f32[16,1792]{1,0:T(8,128)S(1)}, f32[16,1792]{1,0:T(8,128)S(1)}, u32[]{:S(2)}, u32[]{:S(2)}) collective-permute-start(f32[16,1792]{1,0:T(8,128)S(1)} %dynamic-slice_bitcast_fusion), channel_id=1, source_target_pairs={{0,32},{16,48},{32,0},{48,16},{1,33},{17,49},{33,1},{49,17},{2,34}... | collective-permute-start | bytes 344072 | tf_op jit(solution)/shard_map/ppermute | solution.py:214
  62.4 1.1 %collective-permute-start.10 = (f32[3,64,256]{2,1,0:T(8,128)S(1)}, f32[3,64,256]{2,1,0:T(8,128)S(1)}, u32[]{:S(2)}, u32[]{:S(2)}) collective-permute-start(f32[3,64,256]{2,1,0:T(8,128)S(1)} %slice_select_fusion), channel_id=1, source_target_pairs={{0,16},{16,0},{32,48},{48,32},{1,17},{17,1},{33,49},{49,33},{2,18}... | collective-permute-start | bytes 589832 | tf_op jit(solution)/shard_map/ppermute | solution.py:214
  63.6 6.3 %collective-permute-done.20 = f32[16,1792]{1,0:T(8,128)S(1)} collective-permute-done((f32[16,1792]{1,0:T(8,128)S(1)}, f32[16,1792]{1,0:T(8,128)S(1)}, u32[]{:S(2)}, u32[]{:S(2)}) %collective-permute-start.20) | collective-permute-done | bytes 114720 | tf_op jit(solution)/shard_map/ppermute | solution.py:214
  70.0 1.5 %collective-permute-done.10 = f32[3,64,256]{2,1,0:T(8,128)S(1)} collective-permute-done((f32[3,64,256]{2,1,0:T(8,128)S(1)}, f32[3,64,256]{2,1,0:T(8,128)S(1)}, u32[]{:S(2)}, u32[]{:S(2)}) %collective-permute-start.10) | collective-permute-done | bytes 196640 | tf_op jit(solution)/shard_map/ppermute | solution.py:214
  71.6 4.6 %collective-permute-start.11 = (f32[64,256]{1,0:T(8,128)S(1)}, f32[64,256]{1,0:T(8,128)S(1)}, u32[]{:S(2)}, u32[]{:S(2)}) collective-permute-start(f32[64,256]{1,0:T(8,128)S(1)} %get-tuple-element.30), channel_id=1, source_target_pairs={{24,32},{56,64},{88,96},{120,128},{152,160},{184,192},{216,224},{3... | collective-permute-start | bytes 196616 | tf_op jit(solution)/shard_map/ppermute | solution.py:214
  77.0 2.9 %collective-permute-done.11 = f32[64,256]{1,0:T(8,128)S(1)} collective-permute-done((f32[64,256]{1,0:T(8,128)S(1)}, f32[64,256]{1,0:T(8,128)S(1)}, u32[]{:S(2)}, u32[]{:S(2)}) %collective-permute-start.11) | collective-permute-done | bytes 65568 | tf_op jit(solution)/shard_map/ppermute | solution.py:214
  (47 shorter events, 6.5 us)
Async XLA Ops:
  1.6 3.1 %collective-permute-start = (f32[2,2,16,256]{3,2,1,0:T(8,128)S(1)}, f32[2,2,16,256]{3,2,1,0:T(8,128)S(1)}, u32[]{:S(2)}, u32[]{:S(2)}) collective-permute-start(f32[2,2,16,256]{3,2,1,0:T(8,128)S(1)} %get-tuple-element.35), channel_id=1, source_target_pairs={{0,8},{8,0},{1,9},{9,1},{2,10},{10,2},{3,11},{11,3},{4,12},{12,4},... | collective-permute-start | bytes 196616 | tf_op jit(solution)/shard_map/ppermute | solution.py:214
  2.6 6.5 %collective-permute-start.13 = (f32[2,64,256]{2,1,0:T(8,128)S(1)}, f32[2,64,256]{2,1,0:T(8,128)S(1)}, u32[]{:S(2)}, u32[]{:S(2)}) collective-permute-start(f32[2,64,256]{2,1,0:T(8,128)S(1)} %get-tuple-element.15.own), channel_id=1, source_target_pairs={{0,16},{16,0},{32,48},{48,32},{1,17},{17,1},{33,49},{49,33},{2,18}... | collective-permute-start | bytes 393224 | tf_op jit(solution)/shard_map/ppermute | solution.py:214
  4.7 5.5 %collective-permute-start.1 = (f32[4,16,256]{2,1,0:T(8,128)S(1)}, f32[4,16,256]{2,1,0:T(8,128)S(1)}, u32[]{:S(2)}, u32[]{:S(2)}) collective-permute-start(f32[4,16,256]{2,1,0:T(8,128)S(1)} %get-tuple-element.33), channel_id=1, source_target_pairs={{0,16},{16,0},{32,48},{48,32},{1,17},{17,1},{33,49},{49,33},{2,18}... | collective-permute-start | bytes 196616 | tf_op jit(solution)/shard_map/ppermute | solution.py:214
  5.0 15.1 %collective-permute-start.12 = (f32[2,64,256]{2,1,0:T(8,128)S(1)}, f32[2,64,256]{2,1,0:T(8,128)S(1)}, u32[]{:S(2)}, u32[]{:S(2)}) collective-permute-start(f32[2,64,256]{2,1,0:T(8,128)S(1)} %get-tuple-element.15.own), channel_id=1, source_target_pairs={{0,8},{8,0},{1,9},{9,1},{2,10},{10,2},{3,11},{11,3},{4,12},{12,4},... | collective-permute-start | bytes 393224 | tf_op jit(solution)/shard_map/ppermute | solution.py:214
  9.1 11.0 %collective-permute-start.14 = (f32[2,64,256]{2,1,0:T(8,128)S(1)}, f32[2,64,256]{2,1,0:T(8,128)S(1)}, u32[]{:S(2)}, u32[]{:S(2)}) collective-permute-start(f32[2,64,256]{2,1,0:T(8,128)S(1)} %collective-permute-done.13.pair), channel_id=1, source_target_pairs={{0,8},{8,0},{1,9},{9,1},{2,10},{10,2},{3,11},{11,3},{4,12},{12,4},... | collective-permute-start | bytes 393224 | tf_op jit(solution)/shard_map/ppermute | solution.py:214
  10.2 17.5 %collective-permute-start.5 = (f32[8,16,256]{2,1,0:T(8,128)S(1)}, f32[8,16,256]{2,1,0:T(8,128)S(1)}, u32[]{:S(2)}, u32[]{:S(2)}) collective-permute-start(f32[8,16,256]{2,1,0:T(8,128)S(1)} %pad_maximum_fusion.2.refs_0_), channel_id=1, source_target_pairs={{0,1},{1,0},{2,3},{3,2},{4,5},{5,4},{6,7},{7,6},{8,9},{9,8},{10,11... | collective-permute-start | bytes 393224 | tf_op jit(solution)/shard_map/ppermute | solution.py:214
  17.3 11.3 %collective-permute-start.4 = (f32[8,16,256]{2,1,0:T(8,128)S(1)}, f32[8,16,256]{2,1,0:T(8,128)S(1)}, u32[]{:S(2)}, u32[]{:S(2)}) collective-permute-start(f32[8,16,256]{2,1,0:T(8,128)S(1)} %pad_maximum_fusion.2.refs_0_), channel_id=1, source_target_pairs={{0,6},{2,0},{4,2},{6,4},{1,7},{3,1},{5,3},{7,5},{8,14},{10,8},{12,... | collective-permute-start | bytes 393224 | tf_op jit(solution)/shard_map/ppermute | solution.py:214
  20.1 10.9 %collective-permute-start.16 = (f32[64,256]{1,0:T(8,128)S(1)}, f32[64,256]{1,0:T(8,128)S(1)}, u32[]{:S(2)}, u32[]{:S(2)}) collective-permute-start(f32[64,256]{1,0:T(8,128)S(1)} %get-tuple-element.28), channel_id=1, source_target_pairs={{32,0},{40,8},{48,16},{56,24},{64,32},{72,40},{80,48},{88,56},{96,... | collective-permute-start | bytes 196616 | tf_op jit(solution)/shard_map/ppermute | solution.py:214
  23.4 9.1 %collective-permute-start.15 = (f32[64,256]{1,0:T(8,128)S(1)}, f32[64,256]{1,0:T(8,128)S(1)}, u32[]{:S(2)}, u32[]{:S(2)}) collective-permute-start(f32[64,256]{1,0:T(8,128)S(1)} %get-tuple-element.29), channel_id=1, source_target_pairs={{0,32},{8,40},{16,48},{24,56},{32,64},{40,72},{48,80},{56,88},{64,... | collective-permute-start | bytes 196616 | tf_op jit(solution)/shard_map/ppermute | solution.py:214
  26.9 13.1 %collective-permute-start.3 = (f32[8,16,256]{2,1,0:T(8,128)S(1)}, f32[8,16,256]{2,1,0:T(8,128)S(1)}, u32[]{:S(2)}, u32[]{:S(2)}) collective-permute-start(f32[8,16,256]{2,1,0:T(8,128)S(1)} %pad_maximum_fusion.2.refs_0_), channel_id=1, source_target_pairs={{0,4},{2,6},{4,0},{6,2},{1,5},{3,7},{5,1},{7,3},{8,12},{10,14},{12... | collective-permute-start | bytes 393224 | tf_op jit(solution)/shard_map/ppermute | solution.py:214
  27.8 12.2 %collective-permute-start.2 = (f32[8,16,256]{2,1,0:T(8,128)S(1)}, f32[8,16,256]{2,1,0:T(8,128)S(1)}, u32[]{:S(2)}, u32[]{:S(2)}) collective-permute-start(f32[8,16,256]{2,1,0:T(8,128)S(1)} %pad_maximum_fusion.2.refs_0_), channel_id=1, source_target_pairs={{0,2},{2,4},{4,6},{6,0},{1,3},{3,5},{5,7},{7,1},{8,10},{10,12},{12... | collective-permute-start | bytes 393224 | tf_op jit(solution)/shard_map/ppermute | solution.py:214
  28.7 11.3 %collective-permute-start.8 = (f32[8,16,256]{2,1,0:T(8,128)S(1)}, f32[8,16,256]{2,1,0:T(8,128)S(1)}, u32[]{:S(2)}, u32[]{:S(2)}) collective-permute-start(f32[8,16,256]{2,1,0:T(8,128)S(1)} %collective-permute-done.5.refs_4_), channel_id=1, source_target_pairs={{0,6},{2,0},{4,2},{6,4},{1,7},{3,1},{5,3},{7,5},{8,14},{10,8},{12,... | collective-permute-start | bytes 393224 | tf_op jit(solution)/shard_map/ppermute | solution.py:214
  31.0 9.0 %collective-permute-start.7 = (f32[8,16,256]{2,1,0:T(8,128)S(1)}, f32[8,16,256]{2,1,0:T(8,128)S(1)}, u32[]{:S(2)}, u32[]{:S(2)}) collective-permute-start(f32[8,16,256]{2,1,0:T(8,128)S(1)} %collective-permute-done.5.refs_4_), channel_id=1, source_target_pairs={{0,4},{2,6},{4,0},{6,2},{1,5},{3,7},{5,1},{7,3},{8,12},{10,14},{12... | collective-permute-start | bytes 393224 | tf_op jit(solution)/shard_map/ppermute | solution.py:214
  32.5 8.3 %collective-permute-start.6 = (f32[8,16,256]{2,1,0:T(8,128)S(1)}, f32[8,16,256]{2,1,0:T(8,128)S(1)}, u32[]{:S(2)}, u32[]{:S(2)}) collective-permute-start(f32[8,16,256]{2,1,0:T(8,128)S(1)} %collective-permute-done.5.refs_4_), channel_id=1, source_target_pairs={{0,2},{2,4},{4,6},{6,0},{1,3},{3,5},{5,7},{7,1},{8,10},{10,12},{12... | collective-permute-start | bytes 393224 | tf_op jit(solution)/shard_map/ppermute | solution.py:214
  32.6 2.0 %copy-start = (f32[27,64,512]{2,1,0:T(8,128)S(1)}, f32[27,64,512]{2,1,0:T(8,128)}, u32[]{:S(2)}) copy-start(f32[27,64,512]{2,1,0:T(8,128)} %w_ref.1) | copy-start | bytes 10616836
  45.9 14.8 %collective-permute-start.17 = (f32[32,1792]{1,0:T(8,128)S(1)}, f32[32,1792]{1,0:T(8,128)S(1)}, u32[]{:S(2)}, u32[]{:S(2)}) collective-permute-start(f32[32,1792]{1,0:T(8,128)S(1)} %get-tuple-element.19), channel_id=1, source_target_pairs={{0,64},{64,128},{128,192},{192,0},{1,65},{65,129},{129,193},{193,1... | collective-permute-start | bytes 688136 | tf_op jit(solution)/shard_map/ppermute | solution.py:214
  47.5 13.2 %collective-permute-start.18 = (f32[32,1792]{1,0:T(8,128)S(1)}, f32[32,1792]{1,0:T(8,128)S(1)}, u32[]{:S(2)}, u32[]{:S(2)}) collective-permute-start(f32[32,1792]{1,0:T(8,128)S(1)} %get-tuple-element.20), channel_id=1, source_target_pairs={{0,128},{64,192},{128,0},{192,64},{1,129},{65,193},{129,1},{193,65... | collective-permute-start | bytes 688136 | tf_op jit(solution)/shard_map/ppermute | solution.py:214
  48.5 12.3 %collective-permute-start.19 = (f32[32,1792]{1,0:T(8,128)S(1)}, f32[32,1792]{1,0:T(8,128)S(1)}, u32[]{:S(2)}, u32[]{:S(2)}) collective-permute-start(f32[32,1792]{1,0:T(8,128)S(1)} %get-tuple-element.21), channel_id=1, source_target_pairs={{0,192},{64,0},{128,64},{192,128},{1,193},{65,1},{129,65},{193,129... | collective-permute-start | bytes 688136 | tf_op jit(solution)/shard_map/ppermute | solution.py:214
  60.6 1.7 %collective-permute-start.9 = (f32[5,64,256]{2,1,0:T(8,128)S(1)}, f32[5,64,256]{2,1,0:T(8,128)S(1)}, u32[]{:S(2)}, u32[]{:S(2)}) collective-permute-start(f32[5,64,256]{2,1,0:T(8,128)S(1)} %get-tuple-element.13), channel_id=1, source_target_pairs={{0,8},{8,0},{1,9},{9,1},{2,10},{10,2},{3,11},{11,3},{4,12},{12,4},... | collective-permute-start | bytes 983048 | tf_op jit(solution)/shard_map/ppermute | solution.py:214
  60.8 9.1 %collective-permute-start.20 = (f32[16,1792]{1,0:T(8,128)S(1)}, f32[16,1792]{1,0:T(8,128)S(1)}, u32[]{:S(2)}, u32[]{:S(2)}) collective-permute-start(f32[16,1792]{1,0:T(8,128)S(1)} %dynamic-slice_bitcast_fusion), channel_id=1, source_target_pairs={{0,32},{16,48},{32,0},{48,16},{1,33},{17,49},{33,1},{49,17},{2,34}... | collective-permute-start | bytes 344072 | tf_op jit(solution)/shard_map/ppermute | solution.py:214
  62.4 9.1 %collective-permute-start.10 = (f32[3,64,256]{2,1,0:T(8,128)S(1)}, f32[3,64,256]{2,1,0:T(8,128)S(1)}, u32[]{:S(2)}, u32[]{:S(2)}) collective-permute-start(f32[3,64,256]{2,1,0:T(8,128)S(1)} %slice_select_fusion), channel_id=1, source_target_pairs={{0,16},{16,0},{32,48},{48,32},{1,17},{17,1},{33,49},{49,33},{2,18}... | collective-permute-start | bytes 589832 | tf_op jit(solution)/shard_map/ppermute | solution.py:214
  71.6 8.3 %collective-permute-start.11 = (f32[64,256]{1,0:T(8,128)S(1)}, f32[64,256]{1,0:T(8,128)S(1)}, u32[]{:S(2)}, u32[]{:S(2)}) collective-permute-start(f32[64,256]{1,0:T(8,128)S(1)} %get-tuple-element.30), channel_id=1, source_target_pairs={{24,32},{56,64},{88,96},{120,128},{152,160},{184,192},{216,224},{3... | collective-permute-start | bytes 196616 | tf_op jit(solution)/shard_map/ppermute | solution.py:214
